TPU v7x, 1024 devices: a whole 4x4x32 slice. The times are simulated.
1024 devices in a mesh: section: 64 (over z, y_hi), fsdp: 4 (over y_lo, core), tp: 4 (over x).
Axes of the slice: x: 4, y: 4 (y_hi: 2, y_lo: 2; y = y_hi * 2 + y_lo), z: 32, core: 2. Of those that a mesh axis runs over, the one named last changes fastest.
Arguments:
- stash: bfloat16 [64, 4, 512, 2304], P('section', None, 'fsdp'), may hold values from -6 to 6
- grad_now: bfloat16 [64, 512, 2304], P('section', 'fsdp'), may hold values from -6 to 6
- grad_top: bfloat16 [2, 512, 2304], P(None, 'fsdp'), may hold values from -6 to 6
- order: int32 [64, 4], P('section'), may hold values from 0 to 3, each once within a row
- gain: float32 [64, 2304], P('section'), may hold values from 0.5 to 1.5
- weight: bfloat16 [64, 2304, 2048], P('section', 'fsdp', 'tp'), may hold values from -0.125 to 0.125
Outputs:
- grad_held: bfloat16 [64, 512, 2304], P('section', 'fsdp')
- weight_grad: float32 [64, 2304, 2048], P('section', 'fsdp', 'tp')
Inputs may be any that keep to these rules, and one draw needn't show every extreme that they name: Each row of order names every kept micro-batch once.
All inputs are finite; a program needn't handle non-finite values.
Results may differ from a plain program's by a relative error of at most 0.013.
Values may be sent and summed in bfloat16 or wider, within the bound.
No kernel may reach another device: no remote copies, remote signals or barrier semaphores. Data moves between devices by JAX's collectives and lax.ppermute only.
A program may use at most 64 MiB of HBM per device.

v0:
```python
import functools

import jax
import jax.numpy as jnp
from jax import lax
from jax.experimental import pallas as pl
from jax.experimental.pallas import tpu as pltpu
from jax.sharding import PartitionSpec as P


norm_eps = 1e-06
f32 = jnp.float32
bf16 = jnp.bfloat16
gelu_scale = 0.7978845608028654
gelu_cubic = 0.044715
vmem_budget = 16 * 1024 * 1024


def dot_nn(left, right):
    return jnp.dot(left, right, preferred_element_type=f32)


def dot_nt(left, right):
    return lax.dot_general(left, right, (((1,), (1,)), ((), ())), preferred_element_type=f32)


def dot_tn(left, right):
    return lax.dot_general(left, right, (((0,), (0,)), ((), ())), preferred_element_type=f32)


def gelu_and_slope(values):
    squared = values * values
    tanh = jnp.tanh(gelu_scale * values * (1.0 + gelu_cubic * squared))
    half = 0.5 * (1.0 + tanh)
    slope = half + 0.5 * values * (1.0 - tanh * tanh) * (
        gelu_scale * (1.0 + 3.0 * gelu_cubic * squared)
    )
    return values * half, slope


def cost(flops, outs, args):
    size = sum(v.size * v.dtype.itemsize for v in jax.tree.leaves((outs, args)))
    return pl.CostEstimate(flops=int(flops), bytes_accessed=size, transcendentals=0)


def call(kernel, flops, outs, *args):
    return pl.pallas_call(
        kernel,
        out_shape=outs,
        cost_estimate=cost(flops, outs, args),
        compiler_params=pltpu.CompilerParams(vmem_limit_bytes=vmem_budget),
    )(*args)


def cut_blocks(values, ref, first=0):
    count, width = ref.shape[0], ref.shape[2]
    rows = values.shape[0]
    for b in range(count):
        ref[b, first : first + rows] = values[:, b * width : (b + 1) * width]


def normalize(stash_ref, gain_ref, inv_ref):
    values = stash_ref[0, 0].astype(f32)
    inv = lax.rsqrt(jnp.mean(values * values, axis=-1, keepdims=True) + norm_eps)
    inv_ref[...] = jnp.broadcast_to(inv, inv_ref.shape)
    return (values * inv * gain_ref[...]).astype(bf16)


def prepare_first_kernel(order_ref, stash_ref, gain_ref, now_ref, left_ref, x_ref, inv_ref, gain_out):
    cut_blocks(normalize(stash_ref, gain_ref, inv_ref), left_ref)
    cut_blocks(now_ref[0], left_ref, now_ref.shape[1])
    cut_blocks(stash_ref[0, 0], x_ref)
    cut_blocks(gain_ref[...], gain_out)


def prepare_second_kernel(order_ref, stash_ref, gain_ref, top_ref, h_ref, x_ref, inv_ref, top_out):
    cut_blocks(normalize(stash_ref, gain_ref, inv_ref), h_ref)
    cut_blocks(stash_ref[0, 0], x_ref)
    cut_blocks(top_ref[0], top_out)


def first_products(fsdp, left_ref, w_refs):
    total = None
    for j, w_ref in enumerate(w_refs):
        part = dot_nn(left_ref[lax.bitwise_xor(fsdp, j)], w_ref[...])
        total = part if total is None else total + part
    return total


def input_grad(fsdp, grad_pre, w_refs, x_ref, inv_ref, gain_ref, out_ref):
    inv = inv_ref[:, :1]
    moment = jnp.zeros((x_ref.shape[1], 1), f32)
    width = x_ref.shape[2]
    for j, w_ref in enumerate(w_refs):
        block = lax.bitwise_xor(fsdp, j)
        partial_dh = dot_nt(grad_pre, w_ref[...]).astype(bf16)
        scaled = x_ref[block].astype(f32) * inv
        gained = gain_ref[block] * partial_dh.astype(f32)
        moment += jnp.sum(gained * scaled, axis=-1, keepdims=True)
        out_ref[block, :, :width] = partial_dh
    high = moment.astype(bf16)
    low = (moment - high.astype(f32)).astype(bf16)
    rest = out_ref.shape[2] - width
    lane = lax.broadcasted_iota(jnp.int32, (x_ref.shape[1], rest), 1)
    tail = jnp.where(lane == 0, high.astype(f32), jnp.where(lane == 1, low.astype(f32), 0.0))
    for b in range(out_ref.shape[0]):
        out_ref[b, :, width:] = tail.astype(bf16)


def first_kernel(
    left_ref, w0, w1, w2, w3, x_ref, inv_ref, gain_ref, right_ref, out_ref, x_own, dy_own
):
    fsdp = lax.axis_index("fsdp")
    tp = lax.axis_index("tp")
    rows = x_ref.shape[1]
    x_own[...] = x_ref[tp]
    dy_own[...] = left_ref[tp, rows:]
    w_refs = (w0, w1, w2, w3)
    products = first_products(fsdp, left_ref, w_refs)
    activated, slope = gelu_and_slope(products[:rows])
    grad_pre = (slope * products[rows:]).astype(bf16)
    right_ref[:rows] = grad_pre
    right_ref[rows:] = activated.astype(bf16)
    input_grad(fsdp, grad_pre, w_refs, x_ref, inv_ref, gain_ref, out_ref)


def between_kernel(left_ref, right_ref, h_ref, w0, w1, w2, w3, acc_ref, act_ref, slope_ref):
    fsdp = lax.axis_index("fsdp")
    activated, slope = gelu_and_slope(first_products(fsdp, h_ref, (w0, w1, w2, w3)))
    act_ref[...] = activated.astype(bf16)
    slope_ref[...] = slope
    for j in range(acc_ref.shape[0]):
        acc_ref[j] = dot_tn(left_ref[lax.bitwise_xor(fsdp, j)], right_ref[...])


def second_kernel(
    slope_ref, got_ref, top_ref, w0, w1, w2, w3, x_ref, inv_ref, gain_ref,
    dy_ref, pre_ref, out_ref, x_own, dy_own,
):
    fsdp = lax.axis_index("fsdp")
    tp = lax.axis_index("tp")
    is_last = lax.axis_index("section") == lax.axis_size("section") - 1
    w_refs = (w0, w1, w2, w3)
    rows, width = got_ref.shape[1], x_ref.shape[2]

    @pl.when(is_last)
    def _():
        dy_ref[...] = top_ref[...]

    @pl.when(jnp.logical_not(is_last))
    def _():
        dy_ref[:, :rows] = got_ref[:, :, :width]
        dy_ref[:, rows:] = got_ref[:, :, width:]

    x_own[...] = x_ref[tp]
    dy_own[...] = dy_ref[tp]
    backed = first_products(fsdp, dy_ref, w_refs)
    grad_pre = (slope_ref[...] * backed).astype(bf16)
    pre_ref[...] = grad_pre
    input_grad(fsdp, grad_pre, w_refs, x_ref, inv_ref, gain_ref, out_ref)


def share_kernel(count, got_ref, x_ref, inv_ref, gain_ref, dy_ref, out_ref):
    tp = lax.axis_index("tp")
    width = x_ref.shape[1]
    inv = inv_ref[:, :1]
    total = got_ref[0, :, :width].astype(f32)
    tail = got_ref[0, :, width:].astype(f32)
    for b in range(1, got_ref.shape[0]):
        total += got_ref[b, :, :width].astype(f32)
        tail += got_ref[b, :, width:].astype(f32)
    mean = (tail[:, :1] + tail[:, 1:2]) / count
    scaled = x_ref[...].astype(f32) * inv
    gained = gain_ref[tp] * total
    share = (dy_ref[...].astype(f32) + inv * (gained - scaled * mean)).astype(bf16)
    rows = out_ref.shape[0]
    out_ref[:, :width] = share[:rows]
    out_ref[:, width:] = share[rows:]


def late_kernel(h_ref, dy_ref, pre_ref, act_ref, acc_ref, keep_ref, send_ref):
    fsdp = lax.axis_index("fsdp")
    right = jnp.concatenate([pre_ref[...], act_ref[...]], axis=0)
    for j in range(acc_ref.shape[0]):
        block = lax.bitwise_xor(fsdp, j)
        left = jnp.concatenate([h_ref[block], dy_ref[block]], axis=0)
        total = acc_ref[j] + dot_tn(left, right)
        if j % 2:
            send_ref[j // 2] = total.astype(bf16)
        else:
            keep_ref[j // 2] = total


def last_kernel(got_ref, top_ref, out_ref):
    is_last = lax.axis_index("section") == lax.axis_size("section") - 1
    count, rows, width = got_ref.shape[0], got_ref.shape[1], got_ref.shape[2] // 2

    @pl.when(is_last)
    def _():
        out_ref[0] = top_ref[1]

    @pl.when(jnp.logical_not(is_last))
    def _():
        for b in range(count):
            out_ref[0, :rows, b * width : (b + 1) * width] = got_ref[b, :, :width]
            out_ref[0, rows:, b * width : (b + 1) * width] = got_ref[b, :, width:]


def swapped(values, axis, bit):
    return lax.ppermute(values, axis, [(i, i ^ bit) for i in range(lax.axis_size(axis))])


def moved_down(values):
    return lax.ppermute(
        values, "section", [(i, i - 1) for i in range(1, lax.axis_size("section"))]
    )


def exchanged(values):
    return lax.all_to_all(values, "tp", split_axis=0, concat_axis=0, tiled=True)


def copied_to_all(share):
    return exchanged(jnp.broadcast_to(share, (lax.axis_size("tp"), *share.shape)))


def per_device(stash, grad_now, grad_top, order, gain, weight):
    tp_count = lax.axis_size("tp")
    tokens, features = grad_now.shape[1:]
    width = features // tp_count
    inner = weight.shape[2]
    wide = -(-(width + 2) // 128) * 128
    sds = jax.ShapeDtypeStruct

    blocks = sds((tp_count, tokens, width), bf16)
    pairs = sds((tp_count, 2 * tokens, width), bf16)
    flat = sds((tokens, inner), bf16)
    sent = sds((tp_count, tokens, wide), bf16)
    own = [sds((tokens, width), bf16)] * 2
    share = sds((tokens // 2, 2 * width), bf16)
    stats = sds((tokens, 128), f32)
    gain_blocks = sds((tp_count, 1, width), f32)
    own_share = functools.partial(share_kernel, features)
    dot = 2 * tokens * features * inner

    def prepared(kernel, tick, extra, extra_shape, outs):
        whole = [pl.BlockSpec(v.shape, lambda i, slot, n=len(v.shape): (0,) * n) for v in outs]
        return pl.pallas_call(
            kernel,
            grid_spec=pltpu.PrefetchScalarGridSpec(
                num_scalar_prefetch=1,
                grid=(1,),
                in_specs=[
                    pl.BlockSpec((1, 1, tokens, features), lambda i, slot: (0, slot[0, tick], 0, 0)),
                    pl.BlockSpec((1, features), lambda i, slot: (0, 0)),
                    pl.BlockSpec(extra_shape, lambda i, slot: (0, 0, 0)),
                ],
                out_specs=whole,
            ),
            out_shape=outs,
            cost_estimate=cost(dot, outs, (gain,)),
            compiler_params=pltpu.CompilerParams(vmem_limit_bytes=vmem_budget),
        )(order, stash, gain, extra)

    w0 = weight[0]
    w2 = swapped(w0, "fsdp", 2)
    w1 = swapped(w0, "fsdp", 1)
    one = (1, tokens, features)
    left1, x1, inv1, gains = prepared(
        prepare_first_kernel, 0, grad_now, one, [pairs, blocks, stats, gain_blocks]
    )
    h2, x2, inv2, top1 = prepared(
        prepare_second_kernel, 1, grad_top, one, [blocks, blocks, stats, blocks]
    )
    (w2, left1, x1, inv1, gains, h2, x2, inv2, top1) = lax.optimization_barrier(
        (w2, left1, x1, inv1, gains, h2, x2, inv2, top1)
    )
    w3 = swapped(w2, "fsdp", 1)
    weights = (w0, w1, w2, w3)

    right1, out1, x1_own, dy1_own = call(
        first_kernel,
        3 * dot,
        [sds((2 * tokens, inner), bf16), sent, *own],
        left1, *weights, x1, inv1, gains,
    )
    got1 = exchanged(out1)
    share1 = call(own_share, dot // 8, share, got1, x1_own, inv1, gains, dy1_own)
    arrived1 = moved_down(share1)
    acc, act2, slope2 = call(
        between_kernel,
        3 * dot,
        [sds((tp_count, width, inner), f32), flat, sds((tokens, inner), f32)],
        left1, right1, h2, *weights,
    )
    (arrived1, acc, act2, slope2) = lax.optimization_barrier((arrived1, acc, act2, slope2))
    held1 = copied_to_all(arrived1)
    dy2, pre2, out2, x2_own, dy2_own = call(
        second_kernel,
        2 * dot,
        [blocks, flat, sent, *own],
        slope2, held1, top1, *weights, x2, inv2, gains,
    )
    pair = (tp_count // 2, width, inner)
    keep, send = call(
        late_kernel,
        2 * dot,
        [sds(pair, f32), sds(pair, bf16)],
        h2, dy2, pre2, act2, acc,
    )
    (out2, keep, send) = lax.optimization_barrier((out2, keep, send))
    got2 = exchanged(out2)
    share2 = call(own_share, dot // 8, share, got2, x2_own, inv2, gains, dy2_own)
    arrived2 = moved_down(share2)
    from_core = swapped(send, "fsdp", 1)
    across = swapped((keep[1] + from_core[1].astype(f32)).astype(bf16), "fsdp", 2)
    weight_grad = keep[0] + from_core[0].astype(f32) + across.astype(f32)
    held2 = copied_to_all(arrived2)
    grad_held = call(last_kernel, dot // 8, sds((1, tokens, features), bf16), held2, grad_top)
    return (grad_held, weight_grad[None])


def solution(mesh):
    return jax.shard_map(
        per_device,
        mesh=mesh,
        in_specs=(
            P("section", None, "fsdp", None),
            P("section", "fsdp", None),
            P(None, "fsdp", None),
            P("section", None),
            P("section", None),
            P("section", "fsdp", "tp"),
        ),
        out_specs=(P("section", "fsdp", None), P("section", "fsdp", "tp")),
        check_vma=False,
    )
```

profile of v0, /device:TPU:1, one launch (start us, length us, event | category | flops | bytes accessed | tf_op | source)
XLA Modules:
  0.0 105.3 jit_solution(2624625833318462316)
XLA Ops:
  0.6 4.0 %collective-permute-start = (bf16[576,512]{1,0:T(8,128)(2,1)}, bf16[576,512]{1,0:T(8,128)(2,1)S(1)}, u32[]{:S(2)}, u32[]{:S(2)}) collective-permute-start(bf16[576,512]{1,0:T(8,128)(2,1)} %bitcast.9), channel_id=1, source_target_pairs={{0,8},{4,12},{8,0},{12,4},{1,9},{5,13},{9,1},{13,5},{2,10},{6,14},... | collective-permute-start | bytes 1769480 | tf_op jit(solution)/shard_map/ppermute | solution.py:210
  4.7 13.9 %collective-permute-start.1 = (bf16[576,512]{1,0:T(8,128)(2,1)}, bf16[576,512]{1,0:T(8,128)(2,1)S(1)}, u32[]{:S(2)}, u32[]{:S(2)}) collective-permute-start(bf16[576,512]{1,0:T(8,128)(2,1)} %bitcast.10), channel_id=1, source_target_pairs={{0,4},{4,0},{8,12},{12,8},{1,5},{5,1},{9,13},{13,9},{2,6},{6,2},{1... | collective-permute-start | bytes 1769480 | tf_op jit(solution)/shard_map/ppermute | solution.py:210
  18.6 0.0 copy-start
  18.6 1.7 %copy-done = bf16[1,4,128,2304]{3,2,1,0:T(8,128)(2,1)S(1)} copy-done((bf16[1,4,128,2304]{3,2,1,0:T(8,128)(2,1)S(1)}, bf16[1,4,128,2304]{3,2,1,0:T(8,128)(2,1)}, u32[]{:S(2)}) %copy-start) | copy-done | bytes 2359320
  20.3 0.0 copy-start.2
  20.3 1.3 %copy-done.2 = bf16[2,128,2304]{2,1,0:T(8,128)(2,1)S(1)} copy-done((bf16[2,128,2304]{2,1,0:T(8,128)(2,1)S(1)}, bf16[2,128,2304]{2,1,0:T(8,128)(2,1)}, u32[]{:S(2)}) %copy-start.2) | copy-done | bytes 1179672
  21.5 0.0 copy-start.5
  21.5 0.7 copy-done.5
  22.2 0.0 copy-start.6
  22.2 0.7 copy-done.6
  22.9 0.0 copy-start.4
  22.9 1.1 %shard_map.78 = (bf16[4,128,576]{2,1,0:T(8,128)(2,1)S(1)}, bf16[4,128,576]{2,1,0:T(8,128)(2,1)S(1)}, f32[128,128]{1,0:T(8,128)S(1)}, bf16[4,128,576]{2,1,0:T(8,128)(2,1)S(1)}) custom-call(s32[1,4]{1,0:T(1,128)S(1)} %copy-done.6, bf16[1,4,128,2304]{3,2,1,0:T(8,128)(2,1)S(1)} %copy-done, f32[1,2304]{1,0:T(1,128)S(1)} %copy-done.5, ...), custom_call_target="tpu_custom_call" | custom-call | flops 301989888 | bytes 1844224 | tf_op jit(solution)/shard_map/pallas_call | solution.py:248
  24.0 0.0 copy-done.4
  24.0 0.0 copy-start.1
  24.0 1.1 %shard_map.77 = (bf16[4,256,576]{2,1,0:T(8,128)(2,1)S(1)}, bf16[4,128,576]{2,1,0:T(8,128)(2,1)S(1)}, f32[128,128]{1,0:T(8,128)S(1)}, f32[4,1,576]{2,1,0:T(1,128)S(1)}) custom-call(s32[1,4]{1,0:T(1,128)S(1)} %copy-done.6, bf16[1,4,128,2304]{3,2,1,0:T(8,128)(2,1)S(1)} %copy-done, f32[1,2304]{1,0:T(1,128)S(1)} %copy-done.5, bf16[1,128,2304]{2,1,0:T(8,128)(2,1)S(1)} %copy-done.4), custom_call_target="tpu_custom_call" | custom-call | flops 301989888 | bytes 1853440 | tf_op jit(solution)/shard_map/pallas_call | solution.py:248
  25.1 0.0 collective-permute-done.w2
  25.1 3.5 %collective-permute-start.2 = (bf16[576,512]{1,0:T(8,128)(2,1)S(1)}, bf16[576,512]{1,0:T(8,128)(2,1)S(1)}, u32[]{:S(2)}, u32[]{:S(2)}) collective-permute-start(bf16[576,512]{1,0:T(8,128)(2,1)S(1)} %collective-permute-done.w2), channel_id=1, source_target_pairs={{0,4},{4,0},{8,12},{12,8},{1,5},{5,1},{9,13},{13,9},{2,6},{6,2},{1... | collective-permute-start | bytes 1769480 | tf_op jit(solution)/shard_map/ppermute | solution.py:210
  28.6 0.0 collective-permute-done.1.w1
  28.6 1.6 %collective-permute-done.2.w3 = bf16[576,512]{1,0:T(8,128)(2,1)S(1)} collective-permute-done((bf16[576,512]{1,0:T(8,128)(2,1)S(1)}, bf16[576,512]{1,0:T(8,128)(2,1)S(1)}, u32[]{:S(2)}, u32[]{:S(2)}) %collective-permute-start.2) | collective-permute-done | bytes 589856 | tf_op jit(solution)/shard_map/ppermute | solution.py:210
  30.2 0.0 copy-done.1
  30.3 2.1 %shard_map.79 = (bf16[256,512]{1,0:T(8,128)(2,1)S(1)}, bf16[4,128,640]{2,1,0:T(8,128)(2,1)S(1)}, bf16[128,576]{1,0:T(8,128)(2,1)S(1)}, bf16[128,576]{1,0:T(8,128)(2,1)S(1)}) custom-call(bf16[4,256,576]{2,1,0:T(8,128)(2,1)S(1)} %get-tuple-element.48.left_ref, bf16[576,512]{1,0:T(8,128)(2,1)S(1)} %bitcast.11, bf16[576,512]{1,0:T(8,128)(2,1)S(1)} %collective-permute-done.1.w1, ...), custom_call_target="tpu_custom_call" | custom-call | flops 905969664 | bytes 5415936 | tf_op jit(solution)/shard_map/pallas_call | solution.py:47
  32.3 13.0 %all_to_all.20.got_ref = bf16[4,128,640]{2,1,0:T(8,128)(2,1)S(1)} all-to-all(bf16[4,128,640]{2,1,0:T(8,128)(2,1)S(1)} %get-tuple-element.53), channel_id=1, replica_groups=mesh['section'=64,'fsdp'=4,'tp'=4] {'tp'}, dimensions={0} | all-to-all | bytes 1310720 | tf_op jit(solution)/shard_map/all_to_all | solution.py:220
  45.3 0.3 shard_map.80
  45.6 1.3 %collective-permute-start.3 = (bf16[64,1152]{1,0:T(8,128)(2,1)S(1)}, bf16[64,1152]{1,0:T(8,128)(2,1)S(1)}, u32[]{:S(2)}, u32[]{:S(2)}) collective-permute-start(bf16[64,1152]{1,0:T(8,128)(2,1)S(1)} %shard_map.80), channel_id=1, source_target_pairs={{16,0},{32,16},{48,32},{64,48},{80,64},{96,80},{112,96},{128,112},... | collective-permute-start | bytes 442376 | tf_op jit(solution)/shard_map/ppermute | solution.py:214
  46.9 1.3 %shard_map.81 = (f32[4,576,512]{2,1,0:T(8,128)S(1)}, bf16[128,512]{1,0:T(8,128)(2,1)S(1)}, f32[128,512]{1,0:T(8,128)S(1)}) custom-call(bf16[4,256,576]{2,1,0:T(8,128)(2,1)S(1)} %get-tuple-element.48.left_ref, bf16[256,512]{1,0:T(8,128)(2,1)S(1)} %get-tuple-element.56.right_ref, bf16[4,128,576]{2,1,0:T(8,128)(2,1)S(1)} %get-tuple-element.57.h_ref, ...), custom_call_target="tpu_custom_call" | custom-call | flops 905969664 | bytes 9502720 | tf_op jit(solution)/shard_map/pallas_call | solution.py:47
  48.2 4.8 %collective-permute-done.3 = bf16[64,1152]{1,0:T(8,128)(2,1)S(1)} collective-permute-done((bf16[64,1152]{1,0:T(8,128)(2,1)S(1)}, bf16[64,1152]{1,0:T(8,128)(2,1)S(1)}, u32[]{:S(2)}, u32[]{:S(2)}) %collective-permute-start.3) | collective-permute-done | bytes 147488 | tf_op jit(solution)/shard_map/ppermute | solution.py:214
  53.1 10.0 %all_to_all.21.got_ref = bf16[4,64,1152]{2,1,0:T(8,128)(2,1)S(1)} all-to-all(bf16[4,64,1152]{2,1,0:T(8,128)(2,1)S(1)} %broadcast_in_dim.9), channel_id=1, replica_groups=mesh['section'=64,'fsdp'=4,'tp'=4] {'tp'}, dimensions={0} | all-to-all | bytes 1179648 | tf_op jit(solution)/shard_map/all_to_all | solution.py:220
  63.1 1.8 %shard_map.82 = (bf16[4,128,576]{2,1,0:T(8,128)(2,1)S(1)}, bf16[128,512]{1,0:T(8,128)(2,1)S(1)}, bf16[4,128,640]{2,1,0:T(8,128)(2,1)S(1)}, bf16[128,576]{1,0:T(8,128)(2,1)S(1)}, bf16[128,576]{1,0:T(8,128)(2,1)S(1)}) custom-call(f32[128,512]{1,0:T(8,128)S(1)} %get-tuple-element.61.slope_ref, bf16[4,64,1152]{2,1,0:T(8,128)(2,1)S(1)} %all_to_all.21.got_ref, ...), custom_call_target="tpu_custom_call" | custom-call | flops 603979776 | bytes 6136832 | tf_op jit(solution)/shard_map/pallas_call | solution.py:47
  64.9 0.9 shard_map.83
  65.7 5.4 %collective-permute-start.5 = (bf16[2,576,512]{2,1,0:T(8,128)(2,1)S(1)}, bf16[2,576,512]{2,1,0:T(8,128)(2,1)S(1)}, u32[]{:S(2)}, u32[]{:S(2)}) collective-permute-start(bf16[2,576,512]{2,1,0:T(8,128)(2,1)S(1)} %get-tuple-element.77), channel_id=1, source_target_pairs={{0,4},{4,0},{8,12},{12,8},{1,5},{5,1},{9,13},{13,9},{2,6},{6,2},{1... | collective-permute-start | bytes 3538952 | tf_op jit(solution)/shard_map/ppermute | solution.py:210
  71.2 13.1 %all_to_all.22.got_ref = bf16[4,128,640]{2,1,0:T(8,128)(2,1)S(1)} all-to-all(bf16[4,128,640]{2,1,0:T(8,128)(2,1)S(1)} %get-tuple-element.73), channel_id=1, replica_groups=mesh['section'=64,'fsdp'=4,'tp'=4] {'tp'}, dimensions={0} | all-to-all | bytes 1310720 | tf_op jit(solution)/shard_map/all_to_all | solution.py:220
  84.3 0.3 shard_map.84
  84.6 1.3 %collective-permute-start.4 = (bf16[64,1152]{1,0:T(8,128)(2,1)S(1)}, bf16[64,1152]{1,0:T(8,128)(2,1)S(1)}, u32[]{:S(2)}, u32[]{:S(2)}) collective-permute-start(bf16[64,1152]{1,0:T(8,128)(2,1)S(1)} %shard_map.84), channel_id=1, source_target_pairs={{16,0},{32,16},{48,32},{64,48},{80,64},{96,80},{112,96},{128,112},... | collective-permute-start | bytes 442376 | tf_op jit(solution)/shard_map/ppermute | solution.py:214
  85.9 0.0 collective-permute-done.5
  85.9 0.2 fusion.1
  86.1 0.0 copy-start.3
  86.1 2.6 %collective-permute-start.6 = (bf16[576,512]{1,0:T(8,128)(2,1)S(1)}, bf16[576,512]{1,0:T(8,128)(2,1)S(1)}, u32[]{:S(2)}, u32[]{:S(2)}) collective-permute-start(bf16[576,512]{1,0:T(8,128)(2,1)S(1)} %fusion.1), channel_id=1, source_target_pairs={{0,8},{4,12},{8,0},{12,4},{1,9},{5,13},{9,1},{13,5},{2,10},{6,14},... | collective-permute-start | bytes 1769480 | tf_op jit(solution)/shard_map/ppermute | solution.py:210
  88.7 3.3 %collective-permute-done.4 = bf16[64,1152]{1,0:T(8,128)(2,1)S(1)} collective-permute-done((bf16[64,1152]{1,0:T(8,128)(2,1)S(1)}, bf16[64,1152]{1,0:T(8,128)(2,1)S(1)}, u32[]{:S(2)}, u32[]{:S(2)}) %collective-permute-start.4) | collective-permute-done | bytes 147488 | tf_op jit(solution)/shard_map/ppermute | solution.py:214
  92.0 10.3 %all_to_all.23.got_ref = bf16[4,64,1152]{2,1,0:T(8,128)(2,1)S(1)} all-to-all(bf16[4,64,1152]{2,1,0:T(8,128)(2,1)S(1)} %broadcast_in_dim.10), channel_id=1, replica_groups=mesh['section'=64,'fsdp'=4,'tp'=4] {'tp'}, dimensions={0} | all-to-all | bytes 1179648 | tf_op jit(solution)/shard_map/all_to_all | solution.py:220
  102.3 0.0 copy-done.3
  102.3 1.0 shard_map.85
  103.3 0.6 collective-permute-done.6
  104.0 1.3 %fusion = f32[1,576,512]{2,1,0:T(8,128)} fusion(bf16[576,512]{1,0:T(8,128)(2,1)S(1)} %collective-permute-done.6, f32[2,576,512]{2,1,0:T(8,128)S(1)} %get-tuple-element.76, bf16[2,576,512]{2,1,0:T(8,128)(2,1)S(1)} %collective-permute-done.5), kind=kLoop, calls=%fused_computation.1 | loop fusion | flops 1179648 | bytes 3538944 | tf_op jit(solution)/shard_map/broadcast_in_dim | solution.py:320
  (2 shorter events, 0.1 us)
Async XLA Ops:
  0.6 24.5 %collective-permute-start = (bf16[576,512]{1,0:T(8,128)(2,1)}, bf16[576,512]{1,0:T(8,128)(2,1)S(1)}, u32[]{:S(2)}, u32[]{:S(2)}) collective-permute-start(bf16[576,512]{1,0:T(8,128)(2,1)} %bitcast.9), channel_id=1, source_target_pairs={{0,8},{4,12},{8,0},{12,4},{1,9},{5,13},{9,1},{13,5},{2,10},{6,14},... | collective-permute-start | bytes 1769480 | tf_op jit(solution)/shard_map/ppermute | solution.py:210
  4.7 24.0 %collective-permute-start.1 = (bf16[576,512]{1,0:T(8,128)(2,1)}, bf16[576,512]{1,0:T(8,128)(2,1)S(1)}, u32[]{:S(2)}, u32[]{:S(2)}) collective-permute-start(bf16[576,512]{1,0:T(8,128)(2,1)} %bitcast.10), channel_id=1, source_target_pairs={{0,4},{4,0},{8,12},{12,8},{1,5},{5,1},{9,13},{13,9},{2,6},{6,2},{1... | collective-permute-start | bytes 1769480 | tf_op jit(solution)/shard_map/ppermute | solution.py:210
  18.6 1.7 %copy-start = (bf16[1,4,128,2304]{3,2,1,0:T(8,128)(2,1)S(1)}, bf16[1,4,128,2304]{3,2,1,0:T(8,128)(2,1)}, u32[]{:S(2)}) copy-start(bf16[1,4,128,2304]{3,2,1,0:T(8,128)(2,1)} %stash_ref.3) | copy-start | bytes 7077892
  20.3 1.3 %copy-start.2 = (bf16[2,128,2304]{2,1,0:T(8,128)(2,1)S(1)}, bf16[2,128,2304]{2,1,0:T(8,128)(2,1)}, u32[]{:S(2)}) copy-start(bf16[2,128,2304]{2,1,0:T(8,128)(2,1)} %top_ref.3) | copy-start | bytes 3538948
  21.5 0.7 copy-start.5
  22.2 0.7 copy-start.6
  22.9 1.1 %copy-start.4 = (bf16[1,128,2304]{2,1,0:T(8,128)(2,1)S(1)}, bf16[1,128,2304]{2,1,0:T(8,128)(2,1)}, u32[]{:S(2)}) copy-start(bf16[1,128,2304]{2,1,0:T(8,128)(2,1)} %now_ref.1) | copy-start | bytes 1769476
  24.0 6.3 %copy-start.1 = (bf16[1,576,512]{2,1,0:T(8,128)(2,1)S(1)}, bf16[1,576,512]{2,1,0:T(8,128)(2,1)}, u32[]{:S(2)}) copy-start(bf16[1,576,512]{2,1,0:T(8,128)(2,1)} %param.11) | copy-start | bytes 1769476
  25.1 5.1 %collective-permute-start.2 = (bf16[576,512]{1,0:T(8,128)(2,1)S(1)}, bf16[576,512]{1,0:T(8,128)(2,1)S(1)}, u32[]{:S(2)}, u32[]{:S(2)}) collective-permute-start(bf16[576,512]{1,0:T(8,128)(2,1)S(1)} %collective-permute-done.w2), channel_id=1, source_target_pairs={{0,4},{4,0},{8,12},{12,8},{1,5},{5,1},{9,13},{13,9},{2,6},{6,2},{1... | collective-permute-start | bytes 1769480 | tf_op jit(solution)/shard_map/ppermute | solution.py:210
  45.6 7.4 %collective-permute-start.3 = (bf16[64,1152]{1,0:T(8,128)(2,1)S(1)}, bf16[64,1152]{1,0:T(8,128)(2,1)S(1)}, u32[]{:S(2)}, u32[]{:S(2)}) collective-permute-start(bf16[64,1152]{1,0:T(8,128)(2,1)S(1)} %shard_map.80), channel_id=1, source_target_pairs={{16,0},{32,16},{48,32},{64,48},{80,64},{96,80},{112,96},{128,112},... | collective-permute-start | bytes 442376 | tf_op jit(solution)/shard_map/ppermute | solution.py:214
  65.7 20.1 %collective-permute-start.5 = (bf16[2,576,512]{2,1,0:T(8,128)(2,1)S(1)}, bf16[2,576,512]{2,1,0:T(8,128)(2,1)S(1)}, u32[]{:S(2)}, u32[]{:S(2)}) collective-permute-start(bf16[2,576,512]{2,1,0:T(8,128)(2,1)S(1)} %get-tuple-element.77), channel_id=1, source_target_pairs={{0,4},{4,0},{8,12},{12,8},{1,5},{5,1},{9,13},{13,9},{2,6},{6,2},{1... | collective-permute-start | bytes 3538952 | tf_op jit(solution)/shard_map/ppermute | solution.py:210
  84.6 7.4 %collective-permute-start.4 = (bf16[64,1152]{1,0:T(8,128)(2,1)S(1)}, bf16[64,1152]{1,0:T(8,128)(2,1)S(1)}, u32[]{:S(2)}, u32[]{:S(2)}) collective-permute-start(bf16[64,1152]{1,0:T(8,128)(2,1)S(1)} %shard_map.84), channel_id=1, source_target_pairs={{16,0},{32,16},{48,32},{64,48},{80,64},{96,80},{112,96},{128,112},... | collective-permute-start | bytes 442376 | tf_op jit(solution)/shard_map/ppermute | solution.py:214
  86.1 16.2 %copy-start.3 = (bf16[2,128,2304]{2,1,0:T(8,128)(2,1)S(1)}, bf16[2,128,2304]{2,1,0:T(8,128)(2,1)}, u32[]{:S(2)}) copy-start(bf16[2,128,2304]{2,1,0:T(8,128)(2,1)} %top_ref.3) | copy-start | bytes 3538948
  86.1 17.9 %collective-permute-start.6 = (bf16[576,512]{1,0:T(8,128)(2,1)S(1)}, bf16[576,512]{1,0:T(8,128)(2,1)S(1)}, u32[]{:S(2)}, u32[]{:S(2)}) collective-permute-start(bf16[576,512]{1,0:T(8,128)(2,1)S(1)} %fusion.1), channel_id=1, source_target_pairs={{0,8},{4,12},{8,0},{12,4},{1,9},{5,13},{9,1},{13,5},{2,10},{6,14},... | collective-permute-start | bytes 1769480 | tf_op jit(solution)/shard_map/ppermute | solution.py:210
where the time goes:
time: 106 us; the launch traced here: 105 us
  blocking collectives  46.4 us (44%)
  starting transfers between devices  32.1 us (30%)
  waiting for transfers between devices  10.3 us (10%)
  Pallas kernels  9.79 us (9%)
  local copies, waits for them, and re-layouts  4.38 us (4%)
  other arithmetic  1.53 us (1%)
    all_to_all x4, blocking collectives, exchanged(): return lax.all_to_all(values, 'tp', split_axis=0, concat_axis=0, tiled=True)  46.4 us
    ppermute x5, starting transfers between devices, swapped(): lax.ppermute(values, axis, [(i, i ^ bit) for i in range(lax.axis_size(axi...  29.5 us
    ppermute x2, waiting for transfers between devices, moved_down(): lax.ppermute(values, 'section', [(i, i - 1) for i in range(1, lax.axis_si...  8.06 us
    pallas_call x7, Pallas kernels, call(): pl.pallas_call(kernel, out_shape=outs, cost_estimate=cost(flops, outs, ar...  7.6 us
    unnamed x14, local copies, waits for them, and re-layouts  4.3 us
    ppermute x2, starting transfers between devices, moved_down(): lax.ppermute(values, 'section', [(i, i - 1) for i in range(1, lax.axis_si...  2.58 us
    ppermute x5, waiting for transfers between devices, swapped(): lax.ppermute(values, axis, [(i, i ^ bit) for i in range(lax.axis_size(axi...  2.25 us
    pallas_call x2, Pallas kernels, prepared(): pl.pallas_call(kernel, grid_spec=pltpu.PrefetchScalarGridSpec(num_scalar_...  2.19 us
  transfers between devices with their start and end apart: 7, of which 4 were waited for; matrix products, arithmetic and copies ran while one was open for 0% of the time, Pallas kernels for 5%

commit v1 on v0

--- a/solution.py
+++ b/solution.py
@@ -107,16 +107,21 @@
         out_ref[b, :, width:] = tail.astype(bf16)
 
 
+def part_kernel(left_ref, w0, w1, w2, x_ref, part_ref, x_own, dy_own):
+    tp = lax.axis_index("tp")
+    x_own[...] = x_ref[tp]
+    dy_own[...] = left_ref[tp, x_ref.shape[1] :]
+    part_ref[...] = first_products(lax.axis_index("fsdp"), left_ref, (w0, w1, w2))
+
+
 def first_kernel(
-    left_ref, w0, w1, w2, w3, x_ref, inv_ref, gain_ref, right_ref, out_ref, x_own, dy_own
+    part_ref, left_ref, w0, w1, w2, w3, x_ref, inv_ref, gain_ref, right_ref, out_ref
 ):
     fsdp = lax.axis_index("fsdp")
-    tp = lax.axis_index("tp")
     rows = x_ref.shape[1]
-    x_own[...] = x_ref[tp]
-    dy_own[...] = left_ref[tp, rows:]
     w_refs = (w0, w1, w2, w3)
-    products = first_products(fsdp, left_ref, w_refs)
+    last = lax.bitwise_xor(fsdp, len(w_refs) - 1)
+    products = part_ref[...] + dot_nn(left_ref[last], w3[...])
     activated, slope = gelu_and_slope(products[:rows])
     grad_pre = (slope * products[rows:]).astype(bf16)
     right_ref[:rows] = grad_pre
@@ -191,19 +196,28 @@
             keep_ref[j // 2] = total
 
 
-def last_kernel(got_ref, top_ref, out_ref):
+def last_kernel(got_ref, top_ref, keep_ref, core_ref, across_ref, held_ref, grad_ref):
     is_last = lax.axis_index("section") == lax.axis_size("section") - 1
-    count, rows, width = got_ref.shape[0], got_ref.shape[1], got_ref.shape[2] // 2
+    step = pl.program_id(0)
+    count, half_rows, width = got_ref.shape[0], got_ref.shape[1], got_ref.shape[2] // 2
+    rows = held_ref.shape[1]
+    per_half = half_rows // rows
 
     @pl.when(is_last)
     def _():
-        out_ref[0] = top_ref[1]
-
-    @pl.when(jnp.logical_not(is_last))
-    def _():
-        for b in range(count):
-            out_ref[0, :rows, b * width : (b + 1) * width] = got_ref[b, :, :width]
-            out_ref[0, rows:, b * width : (b + 1) * width] = got_ref[b, :, width:]
+        held_ref[...] = top_ref[...]
+
+    for half in range(2):
+
+        @pl.when(jnp.logical_not(is_last) & (step // per_half == half))
+        def _():
+            start = pl.multiple_of(lax.rem(step, per_half) * rows, rows)
+            for b in range(count):
+                held_ref[0, :, b * width : (b + 1) * width] = got_ref[
+                    b, pl.ds(start, rows), half * width : (half + 1) * width
+                ]
+
+    grad_ref[0] = keep_ref[0] + core_ref[0].astype(f32) + across_ref[...].astype(f32)
 
 
 def swapped(values, axis, bit):
@@ -278,11 +292,17 @@
     w3 = swapped(w2, "fsdp", 1)
     weights = (w0, w1, w2, w3)
 
-    right1, out1, x1_own, dy1_own = call(
+    part1, x1_own, dy1_own = call(
+        part_kernel,
+        dot,
+        [sds((2 * tokens, inner), f32), *own],
+        left1, w0, w1, w2, x1,
+    )
+    right1, out1 = call(
         first_kernel,
-        3 * dot,
-        [sds((2 * tokens, inner), bf16), sent, *own],
-        left1, *weights, x1, inv1, gains,
+        2 * dot,
+        [sds((2 * tokens, inner), bf16), sent],
+        part1, left1, *weights, x1, inv1, gains,
     )
     got1 = exchanged(out1)
     share1 = call(own_share, dot // 8, share, got1, x1_own, inv1, gains, dy1_own)
@@ -308,16 +328,33 @@
         [sds(pair, f32), sds(pair, bf16)],
         h2, dy2, pre2, act2, acc,
     )
-    (out2, keep, send) = lax.optimization_barrier((out2, keep, send))
+    from_core = swapped(send, "fsdp", 1)
     got2 = exchanged(out2)
     share2 = call(own_share, dot // 8, share, got2, x2_own, inv2, gains, dy2_own)
     arrived2 = moved_down(share2)
-    from_core = swapped(send, "fsdp", 1)
-    across = swapped((keep[1] + from_core[1].astype(f32)).astype(bf16), "fsdp", 2)
-    weight_grad = keep[0] + from_core[0].astype(f32) + across.astype(f32)
+    across = keep[1] + from_core[1].astype(f32)
+    across = swapped(across.astype(bf16), "fsdp", 2)
     held2 = copied_to_all(arrived2)
-    grad_held = call(last_kernel, dot // 8, sds((1, tokens, features), bf16), held2, grad_top)
-    return (grad_held, weight_grad[None])
+    steps = 4
+    grad_rows = width // steps
+    grad_held, weight_grad = pl.pallas_call(
+        last_kernel,
+        grid=(steps,),
+        in_specs=[
+            pl.BlockSpec(held2.shape, lambda i: (0, 0, 0)),
+            pl.BlockSpec((1, tokens // steps, features), lambda i: (1, i, 0)),
+            pl.BlockSpec((1, grad_rows, inner), lambda i: (0, i, 0)),
+            pl.BlockSpec((1, grad_rows, inner), lambda i: (0, i, 0)),
+            pl.BlockSpec((grad_rows, inner), lambda i: (i, 0)),
+        ],
+        out_specs=[
+            pl.BlockSpec((1, tokens // steps, features), lambda i: (0, i, 0)),
+            pl.BlockSpec((1, grad_rows, inner), lambda i: (0, i, 0)),
+        ],
+        out_shape=[sds((1, tokens, features), bf16), sds((1, width, inner), f32)],
+        compiler_params=pltpu.CompilerParams(vmem_limit_bytes=vmem_budget),
+    )(held2, grad_top, keep, from_core, across)
+    return (grad_held, weight_grad)
 
 
 def solution(mesh):

time: 106 us -> 106 us (level)
  other arithmetic: 1.53 us -> 0.23 us
  Pallas kernels: 9.79 us -> 10.9 us
    pallas_call x0 -> x1, Pallas kernels: none -> 1.98 us  [per_device(): pl.pallas_call(last_kernel, grid=(steps,), in_specs=[pl.BlockSpec(held2.s...]
    broadcast_in_dim x1 -> x0, other arithmetic: 1.3 us -> none  [per_device(): return (grad_held, weight_grad[None])]
  transfers between devices with their start and end apart: 7 -> 7, of which waited for: 4 -> 4; matrix products, arithmetic and copies ran while one was open for 0% -> 0% of each run, Pallas kernels for 5% -> 4%
where the time goes in v1:
time: 106 us; the launch traced here: 105 us
  blocking collectives  46.4 us (44%)
  starting transfers between devices  32.1 us (30%)
  Pallas kernels  10.9 us (10%)
  waiting for transfers between devices  10.5 us (10%)
  local copies, waits for them, and re-layouts  4.38 us (4%)
    all_to_all x4, blocking collectives, exchanged(): return lax.all_to_all(values, 'tp', split_axis=0, concat_axis=0, tiled=True)  46.4 us
    ppermute x5, starting transfers between devices, swapped(): lax.ppermute(values, axis, [(i, i ^ bit) for i in range(lax.axis_size(axi...  29.5 us
    ppermute x2, waiting for transfers between devices, moved_down(): lax.ppermute(values, 'section', [(i, i - 1) for i in range(1, lax.axis_si...  8.06 us
    pallas_call x7, Pallas kernels, call(): pl.pallas_call(kernel, out_shape=outs, cost_estimate=cost(flops, outs, ar...  6.77 us
    unnamed x14, local copies, waits for them, and re-layouts  4.3 us
    ppermute x2, starting transfers between devices, moved_down(): lax.ppermute(values, 'section', [(i, i - 1) for i in range(1, lax.axis_si...  2.58 us
    ppermute x5, waiting for transfers between devices, swapped(): lax.ppermute(values, axis, [(i, i ^ bit) for i in range(lax.axis_size(axi...  2.45 us
    pallas_call x2, Pallas kernels, prepared(): pl.pallas_call(kernel, grid_spec=pltpu.PrefetchScalarGridSpec(num_scalar_...  2.19 us
  transfers between devices with their start and end apart: 7, of which 4 were waited for; matrix products, arithmetic and copies ran while one was open for 0% of the time, Pallas kernels for 4%

profile of v1, /device:TPU:1, one launch (start us, length us, event | category | flops | bytes accessed | tf_op | source)
XLA Modules:
  0.0 105.3 jit_solution(13569379399180251308)
XLA Ops:
  0.6 4.0 %collective-permute-start = (bf16[576,512]{1,0:T(8,128)(2,1)}, bf16[576,512]{1,0:T(8,128)(2,1)S(1)}, u32[]{:S(2)}, u32[]{:S(2)}) collective-permute-start(bf16[576,512]{1,0:T(8,128)(2,1)} %bitcast.3), channel_id=1, source_target_pairs={{0,8},{4,12},{8,0},{12,4},{1,9},{5,13},{9,1},{13,5},{2,10},{6,14},... | collective-permute-start | bytes 1769480 | tf_op jit(solution)/shard_map/ppermute | solution.py:224
  4.7 13.9 %collective-permute-start.1 = (bf16[576,512]{1,0:T(8,128)(2,1)}, bf16[576,512]{1,0:T(8,128)(2,1)S(1)}, u32[]{:S(2)}, u32[]{:S(2)}) collective-permute-start(bf16[576,512]{1,0:T(8,128)(2,1)} %bitcast.4), channel_id=1, source_target_pairs={{0,4},{4,0},{8,12},{12,8},{1,5},{5,1},{9,13},{13,9},{2,6},{6,2},{1... | collective-permute-start | bytes 1769480 | tf_op jit(solution)/shard_map/ppermute | solution.py:224
  18.6 0.0 copy-start.1
  18.6 1.7 %copy-done.1 = bf16[1,4,128,2304]{3,2,1,0:T(8,128)(2,1)S(1)} copy-done((bf16[1,4,128,2304]{3,2,1,0:T(8,128)(2,1)S(1)}, bf16[1,4,128,2304]{3,2,1,0:T(8,128)(2,1)}, u32[]{:S(2)}) %copy-start.1) | copy-done | bytes 2359320
  20.3 0.0 copy-start.2
  20.3 1.3 %copy-done.2 = bf16[2,128,2304]{2,1,0:T(8,128)(2,1)S(1)} copy-done((bf16[2,128,2304]{2,1,0:T(8,128)(2,1)S(1)}, bf16[2,128,2304]{2,1,0:T(8,128)(2,1)}, u32[]{:S(2)}) %copy-start.2) | copy-done | bytes 1179672
  21.5 0.0 copy-start.5
  21.5 0.7 copy-done.5
  22.2 0.0 copy-start.6
  22.2 0.7 copy-done.6
  22.9 0.0 copy-start.4
  22.9 1.1 %shard_map.78 = (bf16[4,128,576]{2,1,0:T(8,128)(2,1)S(1)}, bf16[4,128,576]{2,1,0:T(8,128)(2,1)S(1)}, f32[128,128]{1,0:T(8,128)S(1)}, bf16[4,128,576]{2,1,0:T(8,128)(2,1)S(1)}) custom-call(s32[1,4]{1,0:T(1,128)S(1)} %copy-done.6, bf16[1,4,128,2304]{3,2,1,0:T(8,128)(2,1)S(1)} %copy-done.1, f32[1,2304]{1,0:T(1,128)S(1)} %copy-done.5, ...), custom_call_target="tpu_custom_call" | custom-call | flops 301989888 | bytes 1844224 | tf_op jit(solution)/shard_map/pallas_call | solution.py:262
  24.0 0.0 copy-done.4
  24.0 0.0 copy-start
  24.0 1.1 %shard_map.77 = (bf16[4,256,576]{2,1,0:T(8,128)(2,1)S(1)}, bf16[4,128,576]{2,1,0:T(8,128)(2,1)S(1)}, f32[128,128]{1,0:T(8,128)S(1)}, f32[4,1,576]{2,1,0:T(1,128)S(1)}) custom-call(s32[1,4]{1,0:T(1,128)S(1)} %copy-done.6, bf16[1,4,128,2304]{3,2,1,0:T(8,128)(2,1)S(1)} %copy-done.1, f32[1,2304]{1,0:T(1,128)S(1)} %copy-done.5, bf16[1,128,2304]{2,1,0:T(8,128)(2,1)S(1)} %copy-done.4), custom_call_target="tpu_custom_call" | custom-call | flops 301989888 | bytes 1853440 | tf_op jit(solution)/shard_map/pallas_call | solution.py:262
  25.1 0.0 collective-permute-done.w2
  25.1 3.5 %collective-permute-start.2 = (bf16[576,512]{1,0:T(8,128)(2,1)S(1)}, bf16[576,512]{1,0:T(8,128)(2,1)S(1)}, u32[]{:S(2)}, u32[]{:S(2)}) collective-permute-start(bf16[576,512]{1,0:T(8,128)(2,1)S(1)} %collective-permute-done.w2), channel_id=1, source_target_pairs={{0,4},{4,0},{8,12},{12,8},{1,5},{5,1},{9,13},{13,9},{2,6},{6,2},{1... | collective-permute-start | bytes 1769480 | tf_op jit(solution)/shard_map/ppermute | solution.py:224
  28.6 0.0 collective-permute-done.1.w1
  28.6 0.0 copy-done
  28.7 0.8 shard_map.79
  29.4 0.8 collective-permute-done.2.w3
  30.2 1.5 %shard_map.80 = (bf16[256,512]{1,0:T(8,128)(2,1)S(1)}, bf16[4,128,640]{2,1,0:T(8,128)(2,1)S(1)}) custom-call(f32[256,512]{1,0:T(8,128)S(1)} %get-tuple-element.49.part_ref, bf16[4,256,576]{2,1,0:T(8,128)(2,1)S(1)} %get-tuple-element.46.left_ref, bf16[576,512]{1,0:T(8,128)(2,1)S(1)} %bitcast.6, bf16[576,512]{1,0:T(8,128)(2,1)S(1)} %collective-permute-done.1.w1, ...), custom_call_target="tpu_custom_call" | custom-call | flops 603979776 | bytes 5645312 | tf_op jit(solution)/shard_map/pallas_call | solution.py:47
  31.7 13.0 %all_to_all.20.got_ref = bf16[4,128,640]{2,1,0:T(8,128)(2,1)S(1)} all-to-all(bf16[4,128,640]{2,1,0:T(8,128)(2,1)S(1)} %get-tuple-element.52), channel_id=1, replica_groups=mesh['section'=64,'fsdp'=4,'tp'=4] {'tp'}, dimensions={0} | all-to-all | bytes 1310720 | tf_op jit(solution)/shard_map/all_to_all | solution.py:234
  44.7 0.3 shard_map.81
  45.0 1.3 %collective-permute-start.3 = (bf16[64,1152]{1,0:T(8,128)(2,1)S(1)}, bf16[64,1152]{1,0:T(8,128)(2,1)S(1)}, u32[]{:S(2)}, u32[]{:S(2)}) collective-permute-start(bf16[64,1152]{1,0:T(8,128)(2,1)S(1)} %shard_map.81), channel_id=1, source_target_pairs={{16,0},{32,16},{48,32},{64,48},{80,64},{96,80},{112,96},{128,112},... | collective-permute-start | bytes 442376 | tf_op jit(solution)/shard_map/ppermute | solution.py:228
  46.3 1.3 %shard_map.82 = (f32[4,576,512]{2,1,0:T(8,128)S(1)}, bf16[128,512]{1,0:T(8,128)(2,1)S(1)}, f32[128,512]{1,0:T(8,128)S(1)}) custom-call(bf16[4,256,576]{2,1,0:T(8,128)(2,1)S(1)} %get-tuple-element.46.left_ref, bf16[256,512]{1,0:T(8,128)(2,1)S(1)} %get-tuple-element.55.right_ref, bf16[4,128,576]{2,1,0:T(8,128)(2,1)S(1)} %get-tuple-element.56.h_ref, ...), custom_call_target="tpu_custom_call" | custom-call | flops 905969664 | bytes 9502720 | tf_op jit(solution)/shard_map/pallas_call | solution.py:47
  47.6 4.8 %collective-permute-done.3 = bf16[64,1152]{1,0:T(8,128)(2,1)S(1)} collective-permute-done((bf16[64,1152]{1,0:T(8,128)(2,1)S(1)}, bf16[64,1152]{1,0:T(8,128)(2,1)S(1)}, u32[]{:S(2)}, u32[]{:S(2)}) %collective-permute-start.3) | collective-permute-done | bytes 147488 | tf_op jit(solution)/shard_map/ppermute | solution.py:228
  52.5 10.0 %all_to_all.21.got_ref = bf16[4,64,1152]{2,1,0:T(8,128)(2,1)S(1)} all-to-all(bf16[4,64,1152]{2,1,0:T(8,128)(2,1)S(1)} %broadcast_in_dim.6), channel_id=1, replica_groups=mesh['section'=64,'fsdp'=4,'tp'=4] {'tp'}, dimensions={0} | all-to-all | bytes 1179648 | tf_op jit(solution)/shard_map/all_to_all | solution.py:234
  62.4 1.8 %shard_map.83 = (bf16[4,128,576]{2,1,0:T(8,128)(2,1)S(1)}, bf16[128,512]{1,0:T(8,128)(2,1)S(1)}, bf16[4,128,640]{2,1,0:T(8,128)(2,1)S(1)}, bf16[128,576]{1,0:T(8,128)(2,1)S(1)}, bf16[128,576]{1,0:T(8,128)(2,1)S(1)}) custom-call(f32[128,512]{1,0:T(8,128)S(1)} %get-tuple-element.60.slope_ref, bf16[4,64,1152]{2,1,0:T(8,128)(2,1)S(1)} %all_to_all.21.got_ref, ...), custom_call_target="tpu_custom_call" | custom-call | flops 603979776 | bytes 6136832 | tf_op jit(solution)/shard_map/pallas_call | solution.py:47
  64.2 0.9 shard_map.85
  65.1 5.4 %collective-permute-start.5 = (bf16[2,576,512]{2,1,0:T(8,128)(2,1)S(1)}, bf16[2,576,512]{2,1,0:T(8,128)(2,1)S(1)}, u32[]{:S(2)}, u32[]{:S(2)}) collective-permute-start(bf16[2,576,512]{2,1,0:T(8,128)(2,1)S(1)} %get-tuple-element.73), channel_id=1, source_target_pairs={{0,4},{4,0},{8,12},{12,8},{1,5},{5,1},{9,13},{13,9},{2,6},{6,2},{1... | collective-permute-start | bytes 3538952 | tf_op jit(solution)/shard_map/ppermute | solution.py:224
  70.6 13.1 %all_to_all.22.got_ref = bf16[4,128,640]{2,1,0:T(8,128)(2,1)S(1)} all-to-all(bf16[4,128,640]{2,1,0:T(8,128)(2,1)S(1)} %get-tuple-element.65), channel_id=1, replica_groups=mesh['section'=64,'fsdp'=4,'tp'=4] {'tp'}, dimensions={0} | all-to-all | bytes 1310720 | tf_op jit(solution)/shard_map/all_to_all | solution.py:234
  83.6 0.3 shard_map.84
  83.9 1.3 %collective-permute-start.4 = (bf16[64,1152]{1,0:T(8,128)(2,1)S(1)}, bf16[64,1152]{1,0:T(8,128)(2,1)S(1)}, u32[]{:S(2)}, u32[]{:S(2)}) collective-permute-start(bf16[64,1152]{1,0:T(8,128)(2,1)S(1)} %shard_map.84), channel_id=1, source_target_pairs={{16,0},{32,16},{48,32},{64,48},{80,64},{96,80},{112,96},{128,112},... | collective-permute-start | bytes 442376 | tf_op jit(solution)/shard_map/ppermute | solution.py:228
  85.2 0.0 collective-permute-done.5.core_ref
  85.3 0.2 fusion
  85.5 0.0 copy-start.3
  85.5 2.6 %collective-permute-start.6 = (bf16[576,512]{1,0:T(8,128)(2,1)S(1)}, bf16[576,512]{1,0:T(8,128)(2,1)S(1)}, u32[]{:S(2)}, u32[]{:S(2)}) collective-permute-start(bf16[576,512]{1,0:T(8,128)(2,1)S(1)} %fusion), channel_id=1, source_target_pairs={{0,8},{4,12},{8,0},{12,4},{1,9},{5,13},{9,1},{13,5},{2,10},{6,14},... | collective-permute-start | bytes 1769480 | tf_op jit(solution)/shard_map/ppermute | solution.py:224
  88.1 3.3 %collective-permute-done.4 = bf16[64,1152]{1,0:T(8,128)(2,1)S(1)} collective-permute-done((bf16[64,1152]{1,0:T(8,128)(2,1)S(1)}, bf16[64,1152]{1,0:T(8,128)(2,1)S(1)}, u32[]{:S(2)}, u32[]{:S(2)}) %collective-permute-start.4) | collective-permute-done | bytes 147488 | tf_op jit(solution)/shard_map/ppermute | solution.py:228
  91.4 10.3 %all_to_all.23.got_ref = bf16[4,64,1152]{2,1,0:T(8,128)(2,1)S(1)} all-to-all(bf16[4,64,1152]{2,1,0:T(8,128)(2,1)S(1)} %broadcast_in_dim.7), channel_id=1, replica_groups=mesh['section'=64,'fsdp'=4,'tp'=4] {'tp'}, dimensions={0} | all-to-all | bytes 1179648 | tf_op jit(solution)/shard_map/all_to_all | solution.py:234
  101.7 1.6 %collective-permute-done.6.across_ref = bf16[576,512]{1,0:T(8,128)(2,1)S(1)} collective-permute-done((bf16[576,512]{1,0:T(8,128)(2,1)S(1)}, bf16[576,512]{1,0:T(8,128)(2,1)S(1)}, u32[]{:S(2)}, u32[]{:S(2)}) %collective-permute-start.6) | collective-permute-done | bytes 589856 | tf_op jit(solution)/shard_map/ppermute | solution.py:224
  103.4 0.0 copy-done.3
  103.4 2.0 %shard_map.86 = (bf16[1,128,2304]{2,1,0:T(8,128)(2,1)}, f32[1,576,512]{2,1,0:T(8,128)}) custom-call(bf16[4,64,1152]{2,1,0:T(8,128)(2,1)S(1)} %all_to_all.23.got_ref, bf16[2,128,2304]{2,1,0:T(8,128)(2,1)S(1)} %copy-done.3, f32[2,576,512]{2,1,0:T(8,128)S(1)} %get-tuple-element.72.keep_ref, bf16[2,576,512]{2,1,0:T(8,128)(2,1)S(1)} %collective-permute-done.5.core_ref, ...), custom_call_target="tpu_custom_call" | custom-call | tf_op jit(solution)/shard_map/pallas_call | solution.py:340
  (2 shorter events, 0.1 us)
Async XLA Ops:
  0.6 24.5 %collective-permute-start = (bf16[576,512]{1,0:T(8,128)(2,1)}, bf16[576,512]{1,0:T(8,128)(2,1)S(1)}, u32[]{:S(2)}, u32[]{:S(2)}) collective-permute-start(bf16[576,512]{1,0:T(8,128)(2,1)} %bitcast.3), channel_id=1, source_target_pairs={{0,8},{4,12},{8,0},{12,4},{1,9},{5,13},{9,1},{13,5},{2,10},{6,14},... | collective-permute-start | bytes 1769480 | tf_op jit(solution)/shard_map/ppermute | solution.py:224
  4.7 24.0 %collective-permute-start.1 = (bf16[576,512]{1,0:T(8,128)(2,1)}, bf16[576,512]{1,0:T(8,128)(2,1)S(1)}, u32[]{:S(2)}, u32[]{:S(2)}) collective-permute-start(bf16[576,512]{1,0:T(8,128)(2,1)} %bitcast.4), channel_id=1, source_target_pairs={{0,4},{4,0},{8,12},{12,8},{1,5},{5,1},{9,13},{13,9},{2,6},{6,2},{1... | collective-permute-start | bytes 1769480 | tf_op jit(solution)/shard_map/ppermute | solution.py:224
  18.6 1.7 %copy-start.1 = (bf16[1,4,128,2304]{3,2,1,0:T(8,128)(2,1)S(1)}, bf16[1,4,128,2304]{3,2,1,0:T(8,128)(2,1)}, u32[]{:S(2)}) copy-start(bf16[1,4,128,2304]{3,2,1,0:T(8,128)(2,1)} %stash_ref.3) | copy-start | bytes 7077892
  20.3 1.3 %copy-start.2 = (bf16[2,128,2304]{2,1,0:T(8,128)(2,1)S(1)}, bf16[2,128,2304]{2,1,0:T(8,128)(2,1)}, u32[]{:S(2)}) copy-start(bf16[2,128,2304]{2,1,0:T(8,128)(2,1)} %top_ref.3) | copy-start | bytes 3538948
  21.5 0.7 copy-start.5
  22.2 0.7 copy-start.6
  22.9 1.1 %copy-start.4 = (bf16[1,128,2304]{2,1,0:T(8,128)(2,1)S(1)}, bf16[1,128,2304]{2,1,0:T(8,128)(2,1)}, u32[]{:S(2)}) copy-start(bf16[1,128,2304]{2,1,0:T(8,128)(2,1)} %now_ref.1) | copy-start | bytes 1769476
  24.0 4.7 %copy-start = (bf16[1,576,512]{2,1,0:T(8,128)(2,1)S(1)}, bf16[1,576,512]{2,1,0:T(8,128)(2,1)}, u32[]{:S(2)}) copy-start(bf16[1,576,512]{2,1,0:T(8,128)(2,1)} %param.11) | copy-start | bytes 1769476
  25.1 5.1 %collective-permute-start.2 = (bf16[576,512]{1,0:T(8,128)(2,1)S(1)}, bf16[576,512]{1,0:T(8,128)(2,1)S(1)}, u32[]{:S(2)}, u32[]{:S(2)}) collective-permute-start(bf16[576,512]{1,0:T(8,128)(2,1)S(1)} %collective-permute-done.w2), channel_id=1, source_target_pairs={{0,4},{4,0},{8,12},{12,8},{1,5},{5,1},{9,13},{13,9},{2,6},{6,2},{1... | collective-permute-start | bytes 1769480 | tf_op jit(solution)/shard_map/ppermute | solution.py:224
  45.0 7.4 %collective-permute-start.3 = (bf16[64,1152]{1,0:T(8,128)(2,1)S(1)}, bf16[64,1152]{1,0:T(8,128)(2,1)S(1)}, u32[]{:S(2)}, u32[]{:S(2)}) collective-permute-start(bf16[64,1152]{1,0:T(8,128)(2,1)S(1)} %shard_map.81), channel_id=1, source_target_pairs={{16,0},{32,16},{48,32},{64,48},{80,64},{96,80},{112,96},{128,112},... | collective-permute-start | bytes 442376 | tf_op jit(solution)/shard_map/ppermute | solution.py:228
  65.1 20.1 %collective-permute-start.5 = (bf16[2,576,512]{2,1,0:T(8,128)(2,1)S(1)}, bf16[2,576,512]{2,1,0:T(8,128)(2,1)S(1)}, u32[]{:S(2)}, u32[]{:S(2)}) collective-permute-start(bf16[2,576,512]{2,1,0:T(8,128)(2,1)S(1)} %get-tuple-element.73), channel_id=1, source_target_pairs={{0,4},{4,0},{8,12},{12,8},{1,5},{5,1},{9,13},{13,9},{2,6},{6,2},{1... | collective-permute-start | bytes 3538952 | tf_op jit(solution)/shard_map/ppermute | solution.py:224
  83.9 7.4 %collective-permute-start.4 = (bf16[64,1152]{1,0:T(8,128)(2,1)S(1)}, bf16[64,1152]{1,0:T(8,128)(2,1)S(1)}, u32[]{:S(2)}, u32[]{:S(2)}) collective-permute-start(bf16[64,1152]{1,0:T(8,128)(2,1)S(1)} %shard_map.84), channel_id=1, source_target_pairs={{16,0},{32,16},{48,32},{64,48},{80,64},{96,80},{112,96},{128,112},... | collective-permute-start | bytes 442376 | tf_op jit(solution)/shard_map/ppermute | solution.py:228
  85.5 17.9 %copy-start.3 = (bf16[2,128,2304]{2,1,0:T(8,128)(2,1)S(1)}, bf16[2,128,2304]{2,1,0:T(8,128)(2,1)}, u32[]{:S(2)}) copy-start(bf16[2,128,2304]{2,1,0:T(8,128)(2,1)} %top_ref.3) | copy-start | bytes 3538948
  85.5 17.9 %collective-permute-start.6 = (bf16[576,512]{1,0:T(8,128)(2,1)S(1)}, bf16[576,512]{1,0:T(8,128)(2,1)S(1)}, u32[]{:S(2)}, u32[]{:S(2)}) collective-permute-start(bf16[576,512]{1,0:T(8,128)(2,1)S(1)} %fusion), channel_id=1, source_target_pairs={{0,8},{4,12},{8,0},{12,4},{1,9},{5,13},{9,1},{13,5},{2,10},{6,14},... | collective-permute-start | bytes 1769480 | tf_op jit(solution)/shard_map/ppermute | solution.py:224

commit v2 on v1

--- a/solution.py
+++ b/solution.py
@@ -66,16 +66,28 @@
     return (values * inv * gain_ref[...]).astype(bf16)
 
 
-def prepare_first_kernel(order_ref, stash_ref, gain_ref, now_ref, left_ref, x_ref, inv_ref, gain_out):
+def own_block(values, ref):
+    width = ref.shape[1]
+    for b in range(values.shape[1] // width):
+
+        @pl.when(lax.axis_index("tp") == b)
+        def _():
+            ref[...] = values[:, b * width : (b + 1) * width]
+
+
+def prepare_first_kernel(
+    order_ref, stash_ref, gain_ref, now_ref, left_ref, x_own, inv_ref, dy_own, gain_out
+):
     cut_blocks(normalize(stash_ref, gain_ref, inv_ref), left_ref)
     cut_blocks(now_ref[0], left_ref, now_ref.shape[1])
-    cut_blocks(stash_ref[0, 0], x_ref)
-    cut_blocks(gain_ref[...], gain_out)
-
-
-def prepare_second_kernel(order_ref, stash_ref, gain_ref, top_ref, h_ref, x_ref, inv_ref, top_out):
+    own_block(stash_ref[0, 0], x_own)
+    own_block(now_ref[0], dy_own)
+    own_block(gain_ref[...], gain_out)
+
+
+def prepare_second_kernel(order_ref, stash_ref, gain_ref, top_ref, h_ref, x_own, inv_ref, top_out):
     cut_blocks(normalize(stash_ref, gain_ref, inv_ref), h_ref)
-    cut_blocks(stash_ref[0, 0], x_ref)
+    own_block(stash_ref[0, 0], x_own)
     cut_blocks(top_ref[0], top_out)
 
 
@@ -87,66 +99,57 @@
     return total
 
 
-def input_grad(fsdp, grad_pre, w_refs, x_ref, inv_ref, gain_ref, out_ref):
-    inv = inv_ref[:, :1]
-    moment = jnp.zeros((x_ref.shape[1], 1), f32)
-    width = x_ref.shape[2]
+def input_grad(fsdp, hidden, grad_pre, w_refs, width, out_ref):
     for j, w_ref in enumerate(w_refs):
-        block = lax.bitwise_xor(fsdp, j)
-        partial_dh = dot_nt(grad_pre, w_ref[...]).astype(bf16)
-        scaled = x_ref[block].astype(f32) * inv
-        gained = gain_ref[block] * partial_dh.astype(f32)
-        moment += jnp.sum(gained * scaled, axis=-1, keepdims=True)
-        out_ref[block, :, :width] = partial_dh
+        out_ref[lax.bitwise_xor(fsdp, j), :, :width] = dot_nt(grad_pre, w_ref[...]).astype(bf16)
+    moment = jnp.sum(hidden * grad_pre.astype(f32), axis=-1, keepdims=True)
     high = moment.astype(bf16)
     low = (moment - high.astype(f32)).astype(bf16)
     rest = out_ref.shape[2] - width
-    lane = lax.broadcasted_iota(jnp.int32, (x_ref.shape[1], rest), 1)
+    lane = lax.broadcasted_iota(jnp.int32, (out_ref.shape[1], rest), 1)
     tail = jnp.where(lane == 0, high.astype(f32), jnp.where(lane == 1, low.astype(f32), 0.0))
     for b in range(out_ref.shape[0]):
         out_ref[b, :, width:] = tail.astype(bf16)
 
 
-def part_kernel(left_ref, w0, w1, w2, x_ref, part_ref, x_own, dy_own):
-    tp = lax.axis_index("tp")
-    x_own[...] = x_ref[tp]
-    dy_own[...] = left_ref[tp, x_ref.shape[1] :]
+def part_kernel(left_ref, w0, w1, w2, part_ref):
     part_ref[...] = first_products(lax.axis_index("fsdp"), left_ref, (w0, w1, w2))
 
 
-def first_kernel(
-    part_ref, left_ref, w0, w1, w2, w3, x_ref, inv_ref, gain_ref, right_ref, out_ref
-):
+def first_kernel(part_ref, left_ref, w0, w1, w2, w3, right_ref, out_ref):
     fsdp = lax.axis_index("fsdp")
-    rows = x_ref.shape[1]
+    rows = out_ref.shape[1]
     w_refs = (w0, w1, w2, w3)
     last = lax.bitwise_xor(fsdp, len(w_refs) - 1)
     products = part_ref[...] + dot_nn(left_ref[last], w3[...])
-    activated, slope = gelu_and_slope(products[:rows])
+    hidden = products[:rows]
+    activated, slope = gelu_and_slope(hidden)
     grad_pre = (slope * products[rows:]).astype(bf16)
     right_ref[:rows] = grad_pre
     right_ref[rows:] = activated.astype(bf16)
-    input_grad(fsdp, grad_pre, w_refs, x_ref, inv_ref, gain_ref, out_ref)
-
-
-def between_kernel(left_ref, right_ref, h_ref, w0, w1, w2, w3, acc_ref, act_ref, slope_ref):
+    input_grad(fsdp, hidden, grad_pre, w_refs, left_ref.shape[2], out_ref)
+
+
+def between_kernel(
+    left_ref, right_ref, h_ref, w0, w1, w2, w3, acc_ref, act_ref, hidden_ref, slope_ref
+):
     fsdp = lax.axis_index("fsdp")
-    activated, slope = gelu_and_slope(first_products(fsdp, h_ref, (w0, w1, w2, w3)))
+    hidden = first_products(fsdp, h_ref, (w0, w1, w2, w3))
+    activated, slope = gelu_and_slope(hidden)
     act_ref[...] = activated.astype(bf16)
+    hidden_ref[...] = hidden
     slope_ref[...] = slope
     for j in range(acc_ref.shape[0]):
         acc_ref[j] = dot_tn(left_ref[lax.bitwise_xor(fsdp, j)], right_ref[...])
 
 
 def second_kernel(
-    slope_ref, got_ref, top_ref, w0, w1, w2, w3, x_ref, inv_ref, gain_ref,
-    dy_ref, pre_ref, out_ref, x_own, dy_own,
+    hidden_ref, slope_ref, got_ref, top_ref, w0, w1, w2, w3, dy_ref, pre_ref, out_ref, dy_own
 ):
     fsdp = lax.axis_index("fsdp")
-    tp = lax.axis_index("tp")
     is_last = lax.axis_index("section") == lax.axis_size("section") - 1
     w_refs = (w0, w1, w2, w3)
-    rows, width = got_ref.shape[1], x_ref.shape[2]
+    rows, width = got_ref.shape[1], dy_ref.shape[2]
 
     @pl.when(is_last)
     def _():
@@ -157,16 +160,14 @@
         dy_ref[:, :rows] = got_ref[:, :, :width]
         dy_ref[:, rows:] = got_ref[:, :, width:]
 
-    x_own[...] = x_ref[tp]
-    dy_own[...] = dy_ref[tp]
+    dy_own[...] = dy_ref[lax.axis_index("tp")]
     backed = first_products(fsdp, dy_ref, w_refs)
     grad_pre = (slope_ref[...] * backed).astype(bf16)
     pre_ref[...] = grad_pre
-    input_grad(fsdp, grad_pre, w_refs, x_ref, inv_ref, gain_ref, out_ref)
+    input_grad(fsdp, hidden_ref[...], grad_pre, w_refs, width, out_ref)
 
 
 def share_kernel(count, got_ref, x_ref, inv_ref, gain_ref, dy_ref, out_ref):
-    tp = lax.axis_index("tp")
     width = x_ref.shape[1]
     inv = inv_ref[:, :1]
     total = got_ref[0, :, :width].astype(f32)
@@ -176,7 +177,7 @@
         tail += got_ref[b, :, width:].astype(f32)
     mean = (tail[:, :1] + tail[:, 1:2]) / count
     scaled = x_ref[...].astype(f32) * inv
-    gained = gain_ref[tp] * total
+    gained = gain_ref[...] * total
     share = (dy_ref[...].astype(f32) + inv * (gained - scaled * mean)).astype(bf16)
     rows = out_ref.shape[0]
     out_ref[:, :width] = share[:rows]
@@ -250,10 +251,11 @@
     pairs = sds((tp_count, 2 * tokens, width), bf16)
     flat = sds((tokens, inner), bf16)
     sent = sds((tp_count, tokens, wide), bf16)
-    own = [sds((tokens, width), bf16)] * 2
+    own = sds((tokens, width), bf16)
     share = sds((tokens // 2, 2 * width), bf16)
     stats = sds((tokens, 128), f32)
-    gain_blocks = sds((tp_count, 1, width), f32)
+    gain_own = sds((1, width), f32)
+    high = sds((tokens, inner), f32)
     own_share = functools.partial(share_kernel, features)
     dot = 2 * tokens * features * inner
 
@@ -280,46 +282,40 @@
     w2 = swapped(w0, "fsdp", 2)
     w1 = swapped(w0, "fsdp", 1)
     one = (1, tokens, features)
-    left1, x1, inv1, gains = prepared(
-        prepare_first_kernel, 0, grad_now, one, [pairs, blocks, stats, gain_blocks]
+    left1, x1, inv1, dy1, gains = prepared(
+        prepare_first_kernel, 0, grad_now, one, [pairs, own, stats, own, gain_own]
     )
     h2, x2, inv2, top1 = prepared(
-        prepare_second_kernel, 1, grad_top, one, [blocks, blocks, stats, blocks]
-    )
-    (w2, left1, x1, inv1, gains, h2, x2, inv2, top1) = lax.optimization_barrier(
-        (w2, left1, x1, inv1, gains, h2, x2, inv2, top1)
+        prepare_second_kernel, 1, grad_top, one, [blocks, own, stats, blocks]
+    )
+    (w2, left1, x1, inv1, dy1, gains, h2, x2, inv2, top1) = lax.optimization_barrier(
+        (w2, left1, x1, inv1, dy1, gains, h2, x2, inv2, top1)
     )
     w3 = swapped(w2, "fsdp", 1)
     weights = (w0, w1, w2, w3)
 
-    part1, x1_own, dy1_own = call(
-        part_kernel,
-        dot,
-        [sds((2 * tokens, inner), f32), *own],
-        left1, w0, w1, w2, x1,
-    )
+    part1 = call(part_kernel, dot, sds((2 * tokens, inner), f32), left1, w0, w1, w2)
     right1, out1 = call(
-        first_kernel,
-        2 * dot,
-        [sds((2 * tokens, inner), bf16), sent],
-        part1, left1, *weights, x1, inv1, gains,
+        first_kernel, 2 * dot, [sds((2 * tokens, inner), bf16), sent], part1, left1, *weights
     )
     got1 = exchanged(out1)
-    share1 = call(own_share, dot // 8, share, got1, x1_own, inv1, gains, dy1_own)
+    share1 = call(own_share, dot // 8, share, got1, x1, inv1, gains, dy1)
     arrived1 = moved_down(share1)
-    acc, act2, slope2 = call(
+    acc, act2, hidden2, slope2 = call(
         between_kernel,
         3 * dot,
-        [sds((tp_count, width, inner), f32), flat, sds((tokens, inner), f32)],
+        [sds((tp_count, width, inner), f32), flat, high, high],
         left1, right1, h2, *weights,
     )
-    (arrived1, acc, act2, slope2) = lax.optimization_barrier((arrived1, acc, act2, slope2))
+    (arrived1, acc, act2, hidden2, slope2) = lax.optimization_barrier(
+        (arrived1, acc, act2, hidden2, slope2)
+    )
     held1 = copied_to_all(arrived1)
-    dy2, pre2, out2, x2_own, dy2_own = call(
+    dy2, pre2, out2, dy2_own = call(
         second_kernel,
         2 * dot,
-        [blocks, flat, sent, *own],
-        slope2, held1, top1, *weights, x2, inv2, gains,
+        [blocks, flat, sent, own],
+        hidden2, slope2, held1, top1, *weights,
     )
     pair = (tp_count // 2, width, inner)
     keep, send = call(
@@ -328,10 +324,11 @@
         [sds(pair, f32), sds(pair, bf16)],
         h2, dy2, pre2, act2, acc,
     )
+    (out2, keep, send) = lax.optimization_barrier((out2, keep, send))
+    got2 = exchanged(out2)
+    share2 = call(own_share, dot // 8, share, got2, x2, inv2, gains, dy2_own)
+    arrived2 = moved_down(share2)
     from_core = swapped(send, "fsdp", 1)
-    got2 = exchanged(out2)
-    share2 = call(own_share, dot // 8, share, got2, x2_own, inv2, gains, dy2_own)
-    arrived2 = moved_down(share2)
     across = keep[1] + from_core[1].astype(f32)
     across = swapped(across.astype(bf16), "fsdp", 2)
     held2 = copied_to_all(arrived2)

time: 106 us -> 105 us (level)
  no operation moved by 1% of the time
where the time goes in v2:
time: 105 us
  blocking collectives  46.4 us (44%)
  starting transfers between devices  32 us (30%)
  Pallas kernels  10.5 us (10%)
  waiting for transfers between devices  10.5 us (10%)
  local copies, waits for them, and re-layouts  4.38 us (4%)
    all_to_all x4, blocking collectives, exchanged(): return lax.all_to_all(values, 'tp', split_axis=0, concat_axis=0, tiled=True)  46.4 us
    ppermute x5, starting transfers between devices, swapped(): lax.ppermute(values, axis, [(i, i ^ bit) for i in range(lax.axis_size(axi...  29.5 us
    ppermute x2, waiting for transfers between devices, moved_down(): lax.ppermute(values, 'section', [(i, i - 1) for i in range(1, lax.axis_si...  8.14 us
    pallas_call x7, Pallas kernels, call(): pl.pallas_call(kernel, out_shape=outs, cost_estimate=cost(flops, outs, ar...  6.39 us
    unnamed x14, local copies, waits for them, and re-layouts  4.3 us
    ppermute x2, starting transfers between devices, moved_down(): lax.ppermute(values, 'section', [(i, i - 1) for i in range(1, lax.axis_si...  2.58 us
    ppermute x5, waiting for transfers between devices, swapped(): lax.ppermute(values, axis, [(i, i ^ bit) for i in range(lax.axis_size(axi...  2.32 us
    pallas_call x2, Pallas kernels, prepared(): pl.pallas_call(kernel, grid_spec=pltpu.PrefetchScalarGridSpec(num_scalar_...  2.12 us
  transfers between devices with their start and end apart: 7, of which 4 were waited for; matrix products, arithmetic and copies ran while one was open for 0% of the time, Pallas kernels for 4%

profile of v2, /device:TPU:1, one launch (start us, length us, event | category | flops | bytes accessed | tf_op | source)
XLA Modules:
  0.0 104.8 jit_solution(5965988885314056203)
XLA Ops:
  0.6 4.0 %collective-permute-start = (bf16[576,512]{1,0:T(8,128)(2,1)}, bf16[576,512]{1,0:T(8,128)(2,1)S(1)}, u32[]{:S(2)}, u32[]{:S(2)}) collective-permute-start(bf16[576,512]{1,0:T(8,128)(2,1)} %bitcast.3), channel_id=1, source_target_pairs={{0,8},{4,12},{8,0},{12,4},{1,9},{5,13},{9,1},{13,5},{2,10},{6,14},... | collective-permute-start | bytes 1769480 | tf_op jit(solution)/shard_map/ppermute | solution.py:225
  4.7 13.9 %collective-permute-start.1 = (bf16[576,512]{1,0:T(8,128)(2,1)}, bf16[576,512]{1,0:T(8,128)(2,1)S(1)}, u32[]{:S(2)}, u32[]{:S(2)}) collective-permute-start(bf16[576,512]{1,0:T(8,128)(2,1)} %bitcast.4), channel_id=1, source_target_pairs={{0,4},{4,0},{8,12},{12,8},{1,5},{5,1},{9,13},{13,9},{2,6},{6,2},{1... | collective-permute-start | bytes 1769480 | tf_op jit(solution)/shard_map/ppermute | solution.py:225
  18.6 0.0 copy-start.1
  18.6 1.7 %copy-done.1 = bf16[1,4,128,2304]{3,2,1,0:T(8,128)(2,1)S(1)} copy-done((bf16[1,4,128,2304]{3,2,1,0:T(8,128)(2,1)S(1)}, bf16[1,4,128,2304]{3,2,1,0:T(8,128)(2,1)}, u32[]{:S(2)}) %copy-start.1) | copy-done | bytes 2359320
  20.3 0.0 copy-start.2
  20.3 1.3 %copy-done.2 = bf16[2,128,2304]{2,1,0:T(8,128)(2,1)S(1)} copy-done((bf16[2,128,2304]{2,1,0:T(8,128)(2,1)S(1)}, bf16[2,128,2304]{2,1,0:T(8,128)(2,1)}, u32[]{:S(2)}) %copy-start.2) | copy-done | bytes 1179672
  21.5 0.0 copy-start.5
  21.5 0.7 copy-done.5
  22.2 0.0 copy-start.6
  22.2 0.7 copy-done.6
  22.9 0.0 copy-start.4
  22.9 1.1 %shard_map.78 = (bf16[4,128,576]{2,1,0:T(8,128)(2,1)S(1)}, bf16[128,576]{1,0:T(8,128)(2,1)S(1)}, f32[128,128]{1,0:T(8,128)S(1)}, bf16[4,128,576]{2,1,0:T(8,128)(2,1)S(1)}) custom-call(s32[1,4]{1,0:T(1,128)S(1)} %copy-done.6, bf16[1,4,128,2304]{3,2,1,0:T(8,128)(2,1)S(1)} %copy-done.1, f32[1,2304]{1,0:T(1,128)S(1)} %copy-done.5, ...), custom_call_target="tpu_custom_call" | custom-call | flops 301989888 | bytes 1401856 | tf_op jit(solution)/shard_map/pallas_call | solution.py:264
  24.0 0.0 copy-done.4
  24.0 0.0 copy-start
  24.0 1.1 %shard_map.77 = (bf16[4,256,576]{2,1,0:T(8,128)(2,1)S(1)}, bf16[128,576]{1,0:T(8,128)(2,1)S(1)}, f32[128,128]{1,0:T(8,128)S(1)}, bf16[128,576]{1,0:T(8,128)(2,1)S(1)}, f32[1,576]{1,0:T(1,128)S(1)}) custom-call(s32[1,4]{1,0:T(1,128)S(1)} %copy-done.6, bf16[1,4,128,2304]{3,2,1,0:T(8,128)(2,1)S(1)} %copy-done.1, f32[1,2304]{1,0:T(1,128)S(1)} %copy-done.5, ...), custom_call_target="tpu_custom_call" | custom-call | flops 301989888 | bytes 1551616 | tf_op jit(solution)/shard_map/pallas_call | solution.py:264
  25.0 0.0 collective-permute-done.w2
  25.1 3.6 %collective-permute-start.2 = (bf16[576,512]{1,0:T(8,128)(2,1)S(1)}, bf16[576,512]{1,0:T(8,128)(2,1)S(1)}, u32[]{:S(2)}, u32[]{:S(2)}) collective-permute-start(bf16[576,512]{1,0:T(8,128)(2,1)S(1)} %collective-permute-done.w2), channel_id=1, source_target_pairs={{0,4},{4,0},{8,12},{12,8},{1,5},{5,1},{9,13},{13,9},{2,6},{6,2},{1... | collective-permute-start | bytes 1769480 | tf_op jit(solution)/shard_map/ppermute | solution.py:225
  28.6 0.0 collective-permute-done.1.w1
  28.6 0.0 copy-done
  28.7 0.8 shard_map.79.part_ref
  29.4 0.8 collective-permute-done.2.w3
  30.2 1.3 %shard_map.80 = (bf16[256,512]{1,0:T(8,128)(2,1)S(1)}, bf16[4,128,640]{2,1,0:T(8,128)(2,1)S(1)}) custom-call(f32[256,512]{1,0:T(8,128)S(1)} %shard_map.79.part_ref, bf16[4,256,576]{2,1,0:T(8,128)(2,1)S(1)} %get-tuple-element.50.left_ref, bf16[576,512]{1,0:T(8,128)(2,1)S(1)} %bitcast.6, bf16[576,512]{1,0:T(8,128)(2,1)S(1)} %collective-permute-done.1.w1, ...), custom_call_target="tpu_custom_call" | custom-call | flops 603979776 | bytes 4980736 | tf_op jit(solution)/shard_map/pallas_call | solution.py:47
  31.6 13.0 %all_to_all.20.got_ref = bf16[4,128,640]{2,1,0:T(8,128)(2,1)S(1)} all-to-all(bf16[4,128,640]{2,1,0:T(8,128)(2,1)S(1)} %get-tuple-element.52), channel_id=1, replica_groups=mesh['section'=64,'fsdp'=4,'tp'=4] {'tp'}, dimensions={0} | all-to-all | bytes 1310720 | tf_op jit(solution)/shard_map/all_to_all | solution.py:235
  44.6 0.3 shard_map.81
  44.9 1.3 %collective-permute-start.3 = (bf16[64,1152]{1,0:T(8,128)(2,1)S(1)}, bf16[64,1152]{1,0:T(8,128)(2,1)S(1)}, u32[]{:S(2)}, u32[]{:S(2)}) collective-permute-start(bf16[64,1152]{1,0:T(8,128)(2,1)S(1)} %shard_map.81), channel_id=1, source_target_pairs={{16,0},{32,16},{48,32},{64,48},{80,64},{96,80},{112,96},{128,112},... | collective-permute-start | bytes 442376 | tf_op jit(solution)/shard_map/ppermute | solution.py:229
  46.2 1.3 %shard_map.82 = (f32[4,576,512]{2,1,0:T(8,128)S(1)}, bf16[128,512]{1,0:T(8,128)(2,1)S(1)}, f32[128,512]{1,0:T(8,128)S(1)}, f32[128,512]{1,0:T(8,128)S(1)}) custom-call(bf16[4,256,576]{2,1,0:T(8,128)(2,1)S(1)} %get-tuple-element.50.left_ref, bf16[256,512]{1,0:T(8,128)(2,1)S(1)} %get-tuple-element.57.right_ref, ...), custom_call_target="tpu_custom_call" | custom-call | flops 905969664 | bytes 9764864 | tf_op jit(solution)/shard_map/pallas_call | solution.py:47
  47.5 4.8 %collective-permute-done.3 = bf16[64,1152]{1,0:T(8,128)(2,1)S(1)} collective-permute-done((bf16[64,1152]{1,0:T(8,128)(2,1)S(1)}, bf16[64,1152]{1,0:T(8,128)(2,1)S(1)}, u32[]{:S(2)}, u32[]{:S(2)}) %collective-permute-start.3) | collective-permute-done | bytes 147488 | tf_op jit(solution)/shard_map/ppermute | solution.py:229
  52.3 10.0 %all_to_all.21.got_ref = bf16[4,64,1152]{2,1,0:T(8,128)(2,1)S(1)} all-to-all(bf16[4,64,1152]{2,1,0:T(8,128)(2,1)S(1)} %broadcast_in_dim.6), channel_id=1, replica_groups=mesh['section'=64,'fsdp'=4,'tp'=4] {'tp'}, dimensions={0} | all-to-all | bytes 1179648 | tf_op jit(solution)/shard_map/all_to_all | solution.py:235
  62.3 1.6 %shard_map.83 = (bf16[4,128,576]{2,1,0:T(8,128)(2,1)S(1)}, bf16[128,512]{1,0:T(8,128)(2,1)S(1)}, bf16[4,128,640]{2,1,0:T(8,128)(2,1)S(1)}, bf16[128,576]{1,0:T(8,128)(2,1)S(1)}) custom-call(f32[128,512]{1,0:T(8,128)S(1)} %get-tuple-element.63.hidden_ref, f32[128,512]{1,0:T(8,128)S(1)} %get-tuple-element.64.slope_ref, ...), custom_call_target="tpu_custom_call" | custom-call | flops 603979776 | bytes 5586944 | tf_op jit(solution)/shard_map/pallas_call | solution.py:47
  63.9 0.8 shard_map.84
  64.8 5.4 %collective-permute-start.5 = (bf16[2,576,512]{2,1,0:T(8,128)(2,1)S(1)}, bf16[2,576,512]{2,1,0:T(8,128)(2,1)S(1)}, u32[]{:S(2)}, u32[]{:S(2)}) collective-permute-start(bf16[2,576,512]{2,1,0:T(8,128)(2,1)S(1)} %get-tuple-element.79), channel_id=1, source_target_pairs={{0,4},{4,0},{8,12},{12,8},{1,5},{5,1},{9,13},{13,9},{2,6},{6,2},{1... | collective-permute-start | bytes 3538952 | tf_op jit(solution)/shard_map/ppermute | solution.py:225
  70.2 13.1 %all_to_all.22.got_ref = bf16[4,128,640]{2,1,0:T(8,128)(2,1)S(1)} all-to-all(bf16[4,128,640]{2,1,0:T(8,128)(2,1)S(1)} %get-tuple-element.74), channel_id=1, replica_groups=mesh['section'=64,'fsdp'=4,'tp'=4] {'tp'}, dimensions={0} | all-to-all | bytes 1310720 | tf_op jit(solution)/shard_map/all_to_all | solution.py:235
  83.3 0.3 shard_map.85
  83.6 1.3 %collective-permute-start.4 = (bf16[64,1152]{1,0:T(8,128)(2,1)S(1)}, bf16[64,1152]{1,0:T(8,128)(2,1)S(1)}, u32[]{:S(2)}, u32[]{:S(2)}) collective-permute-start(bf16[64,1152]{1,0:T(8,128)(2,1)S(1)} %shard_map.85), channel_id=1, source_target_pairs={{16,0},{32,16},{48,32},{64,48},{80,64},{96,80},{112,96},{128,112},... | collective-permute-start | bytes 442376 | tf_op jit(solution)/shard_map/ppermute | solution.py:229
  84.9 0.0 collective-permute-done.5.core_ref
  84.9 0.2 fusion
  85.1 0.0 copy-start.3
  85.1 2.5 %collective-permute-start.6 = (bf16[576,512]{1,0:T(8,128)(2,1)S(1)}, bf16[576,512]{1,0:T(8,128)(2,1)S(1)}, u32[]{:S(2)}, u32[]{:S(2)}) collective-permute-start(bf16[576,512]{1,0:T(8,128)(2,1)S(1)} %fusion), channel_id=1, source_target_pairs={{0,8},{4,12},{8,0},{12,4},{1,9},{5,13},{9,1},{13,5},{2,10},{6,14},... | collective-permute-start | bytes 1769480 | tf_op jit(solution)/shard_map/ppermute | solution.py:225
  87.7 3.3 %collective-permute-done.4 = bf16[64,1152]{1,0:T(8,128)(2,1)S(1)} collective-permute-done((bf16[64,1152]{1,0:T(8,128)(2,1)S(1)}, bf16[64,1152]{1,0:T(8,128)(2,1)S(1)}, u32[]{:S(2)}, u32[]{:S(2)}) %collective-permute-start.4) | collective-permute-done | bytes 147488 | tf_op jit(solution)/shard_map/ppermute | solution.py:229
  91.0 10.3 %all_to_all.23.got_ref = bf16[4,64,1152]{2,1,0:T(8,128)(2,1)S(1)} all-to-all(bf16[4,64,1152]{2,1,0:T(8,128)(2,1)S(1)} %broadcast_in_dim.7), channel_id=1, replica_groups=mesh['section'=64,'fsdp'=4,'tp'=4] {'tp'}, dimensions={0} | all-to-all | bytes 1179648 | tf_op jit(solution)/shard_map/all_to_all | solution.py:235
  101.4 1.5 %collective-permute-done.6.across_ref = bf16[576,512]{1,0:T(8,128)(2,1)S(1)} collective-permute-done((bf16[576,512]{1,0:T(8,128)(2,1)S(1)}, bf16[576,512]{1,0:T(8,128)(2,1)S(1)}, u32[]{:S(2)}, u32[]{:S(2)}) %collective-permute-start.6) | collective-permute-done | bytes 589856 | tf_op jit(solution)/shard_map/ppermute | solution.py:225
  102.9 0.0 copy-done.3
  102.9 2.0 %shard_map.86 = (bf16[1,128,2304]{2,1,0:T(8,128)(2,1)}, f32[1,576,512]{2,1,0:T(8,128)}) custom-call(bf16[4,64,1152]{2,1,0:T(8,128)(2,1)S(1)} %all_to_all.23.got_ref, bf16[2,128,2304]{2,1,0:T(8,128)(2,1)S(1)} %copy-done.3, f32[2,576,512]{2,1,0:T(8,128)S(1)} %get-tuple-element.78.keep_ref, bf16[2,576,512]{2,1,0:T(8,128)(2,1)S(1)} %collective-permute-done.5.core_ref, ...), custom_call_target="tpu_custom_call" | custom-call | tf_op jit(solution)/shard_map/pallas_call | solution.py:337
  (2 shorter events, 0.1 us)
Async XLA Ops:
  0.6 24.4 %collective-permute-start = (bf16[576,512]{1,0:T(8,128)(2,1)}, bf16[576,512]{1,0:T(8,128)(2,1)S(1)}, u32[]{:S(2)}, u32[]{:S(2)}) collective-permute-start(bf16[576,512]{1,0:T(8,128)(2,1)} %bitcast.3), channel_id=1, source_target_pairs={{0,8},{4,12},{8,0},{12,4},{1,9},{5,13},{9,1},{13,5},{2,10},{6,14},... | collective-permute-start | bytes 1769480 | tf_op jit(solution)/shard_map/ppermute | solution.py:225
  4.7 24.0 %collective-permute-start.1 = (bf16[576,512]{1,0:T(8,128)(2,1)}, bf16[576,512]{1,0:T(8,128)(2,1)S(1)}, u32[]{:S(2)}, u32[]{:S(2)}) collective-permute-start(bf16[576,512]{1,0:T(8,128)(2,1)} %bitcast.4), channel_id=1, source_target_pairs={{0,4},{4,0},{8,12},{12,8},{1,5},{5,1},{9,13},{13,9},{2,6},{6,2},{1... | collective-permute-start | bytes 1769480 | tf_op jit(solution)/shard_map/ppermute | solution.py:225
  18.6 1.7 %copy-start.1 = (bf16[1,4,128,2304]{3,2,1,0:T(8,128)(2,1)S(1)}, bf16[1,4,128,2304]{3,2,1,0:T(8,128)(2,1)}, u32[]{:S(2)}) copy-start(bf16[1,4,128,2304]{3,2,1,0:T(8,128)(2,1)} %stash_ref.3) | copy-start | bytes 7077892
  20.3 1.3 %copy-start.2 = (bf16[2,128,2304]{2,1,0:T(8,128)(2,1)S(1)}, bf16[2,128,2304]{2,1,0:T(8,128)(2,1)}, u32[]{:S(2)}) copy-start(bf16[2,128,2304]{2,1,0:T(8,128)(2,1)} %top_ref.3) | copy-start | bytes 3538948
  21.5 0.7 copy-start.5
  22.2 0.7 copy-start.6
  22.9 1.1 %copy-start.4 = (bf16[1,128,2304]{2,1,0:T(8,128)(2,1)S(1)}, bf16[1,128,2304]{2,1,0:T(8,128)(2,1)}, u32[]{:S(2)}) copy-start(bf16[1,128,2304]{2,1,0:T(8,128)(2,1)} %now_ref.1) | copy-start | bytes 1769476
  24.0 4.7 %copy-start = (bf16[1,576,512]{2,1,0:T(8,128)(2,1)S(1)}, bf16[1,576,512]{2,1,0:T(8,128)(2,1)}, u32[]{:S(2)}) copy-start(bf16[1,576,512]{2,1,0:T(8,128)(2,1)} %param.11) | copy-start | bytes 1769476
  25.1 5.2 %collective-permute-start.2 = (bf16[576,512]{1,0:T(8,128)(2,1)S(1)}, bf16[576,512]{1,0:T(8,128)(2,1)S(1)}, u32[]{:S(2)}, u32[]{:S(2)}) collective-permute-start(bf16[576,512]{1,0:T(8,128)(2,1)S(1)} %collective-permute-done.w2), channel_id=1, source_target_pairs={{0,4},{4,0},{8,12},{12,8},{1,5},{5,1},{9,13},{13,9},{2,6},{6,2},{1... | collective-permute-start | bytes 1769480 | tf_op jit(solution)/shard_map/ppermute | solution.py:225
  44.9 7.4 %collective-permute-start.3 = (bf16[64,1152]{1,0:T(8,128)(2,1)S(1)}, bf16[64,1152]{1,0:T(8,128)(2,1)S(1)}, u32[]{:S(2)}, u32[]{:S(2)}) collective-permute-start(bf16[64,1152]{1,0:T(8,128)(2,1)S(1)} %shard_map.81), channel_id=1, source_target_pairs={{16,0},{32,16},{48,32},{64,48},{80,64},{96,80},{112,96},{128,112},... | collective-permute-start | bytes 442376 | tf_op jit(solution)/shard_map/ppermute | solution.py:229
  64.8 20.1 %collective-permute-start.5 = (bf16[2,576,512]{2,1,0:T(8,128)(2,1)S(1)}, bf16[2,576,512]{2,1,0:T(8,128)(2,1)S(1)}, u32[]{:S(2)}, u32[]{:S(2)}) collective-permute-start(bf16[2,576,512]{2,1,0:T(8,128)(2,1)S(1)} %get-tuple-element.79), channel_id=1, source_target_pairs={{0,4},{4,0},{8,12},{12,8},{1,5},{5,1},{9,13},{13,9},{2,6},{6,2},{1... | collective-permute-start | bytes 3538952 | tf_op jit(solution)/shard_map/ppermute | solution.py:225
  83.6 7.4 %collective-permute-start.4 = (bf16[64,1152]{1,0:T(8,128)(2,1)S(1)}, bf16[64,1152]{1,0:T(8,128)(2,1)S(1)}, u32[]{:S(2)}, u32[]{:S(2)}) collective-permute-start(bf16[64,1152]{1,0:T(8,128)(2,1)S(1)} %shard_map.85), channel_id=1, source_target_pairs={{16,0},{32,16},{48,32},{64,48},{80,64},{96,80},{112,96},{128,112},... | collective-permute-start | bytes 442376 | tf_op jit(solution)/shard_map/ppermute | solution.py:229
  85.1 17.7 %copy-start.3 = (bf16[2,128,2304]{2,1,0:T(8,128)(2,1)S(1)}, bf16[2,128,2304]{2,1,0:T(8,128)(2,1)}, u32[]{:S(2)}) copy-start(bf16[2,128,2304]{2,1,0:T(8,128)(2,1)} %top_ref.3) | copy-start | bytes 3538948
  85.1 17.7 %collective-permute-start.6 = (bf16[576,512]{1,0:T(8,128)(2,1)S(1)}, bf16[576,512]{1,0:T(8,128)(2,1)S(1)}, u32[]{:S(2)}, u32[]{:S(2)}) collective-permute-start(bf16[576,512]{1,0:T(8,128)(2,1)S(1)} %fusion), channel_id=1, source_target_pairs={{0,8},{4,12},{8,0},{12,4},{1,9},{5,13},{9,1},{13,5},{2,10},{6,14},... | collective-permute-start | bytes 1769480 | tf_op jit(solution)/shard_map/ppermute | solution.py:225

commit v3 on v2

--- a/solution.py
+++ b/solution.py
@@ -197,27 +197,22 @@
             keep_ref[j // 2] = total
 
 
-def last_kernel(got_ref, top_ref, keep_ref, core_ref, across_ref, held_ref, grad_ref):
+def last_kernel(got_ref, top_ref, held_ref):
     is_last = lax.axis_index("section") == lax.axis_size("section") - 1
-    step = pl.program_id(0)
-    count, half_rows, width = got_ref.shape[0], got_ref.shape[1], got_ref.shape[2] // 2
-    rows = held_ref.shape[1]
-    per_half = half_rows // rows
+    count, rows, width = got_ref.shape[0], got_ref.shape[1], got_ref.shape[2] // 2
 
     @pl.when(is_last)
     def _():
-        held_ref[...] = top_ref[...]
-
-    for half in range(2):
-
-        @pl.when(jnp.logical_not(is_last) & (step // per_half == half))
-        def _():
-            start = pl.multiple_of(lax.rem(step, per_half) * rows, rows)
-            for b in range(count):
-                held_ref[0, :, b * width : (b + 1) * width] = got_ref[
-                    b, pl.ds(start, rows), half * width : (half + 1) * width
-                ]
-
+        held_ref[0] = top_ref[1]
+
+    @pl.when(jnp.logical_not(is_last))
+    def _():
+        for b in range(count):
+            held_ref[0, :rows, b * width : (b + 1) * width] = got_ref[b, :, :width]
+            held_ref[0, rows:, b * width : (b + 1) * width] = got_ref[b, :, width:]
+
+
+def join_kernel(keep_ref, core_ref, across_ref, grad_ref):
     grad_ref[0] = keep_ref[0] + core_ref[0].astype(f32) + across_ref[...].astype(f32)
 
 
@@ -332,25 +327,21 @@
     across = keep[1] + from_core[1].astype(f32)
     across = swapped(across.astype(bf16), "fsdp", 2)
     held2 = copied_to_all(arrived2)
-    steps = 4
+    grad_held = call(last_kernel, dot // 8, sds((1, tokens, features), bf16), held2, grad_top)
+    steps = 3
     grad_rows = width // steps
-    grad_held, weight_grad = pl.pallas_call(
-        last_kernel,
+    weight_grad = pl.pallas_call(
+        join_kernel,
         grid=(steps,),
         in_specs=[
-            pl.BlockSpec(held2.shape, lambda i: (0, 0, 0)),
-            pl.BlockSpec((1, tokens // steps, features), lambda i: (1, i, 0)),
             pl.BlockSpec((1, grad_rows, inner), lambda i: (0, i, 0)),
             pl.BlockSpec((1, grad_rows, inner), lambda i: (0, i, 0)),
             pl.BlockSpec((grad_rows, inner), lambda i: (i, 0)),
         ],
-        out_specs=[
-            pl.BlockSpec((1, tokens // steps, features), lambda i: (0, i, 0)),
-            pl.BlockSpec((1, grad_rows, inner), lambda i: (0, i, 0)),
-        ],
-        out_shape=[sds((1, tokens, features), bf16), sds((1, width, inner), f32)],
+        out_specs=pl.BlockSpec((1, grad_rows, inner), lambda i: (0, i, 0)),
+        out_shape=sds((1, width, inner), f32),
         compiler_params=pltpu.CompilerParams(vmem_limit_bytes=vmem_budget),
-    )(held2, grad_top, keep, from_core, across)
+    )(keep, from_core, across)
     return (grad_held, weight_grad)
 
 

time: 105 us -> 106 us (level); the launches traced: 105 us -> 105 us
    pallas_call x7 -> x8, Pallas kernels: 6.39 us -> 7.37 us  [call(): pl.pallas_call(kernel, out_shape=outs, cost_estimate=cost(flops, outs, ar...]
  transfers between devices with their start and end apart: 7 -> 7, of which waited for: 4 -> 4; matrix products, arithmetic and copies ran while one was open for 0% -> 0% of each run, Pallas kernels for 4% -> 5%
where the time goes in v3:
time: 106 us; the launch traced here: 105 us
  blocking collectives  46.4 us (44%)
  starting transfers between devices  32 us (30%)
  Pallas kernels  11.1 us (10%)
  waiting for transfers between devices  9.55 us (9%)
  local copies, waits for them, and re-layouts  4.38 us (4%)
    all_to_all x4, blocking collectives, exchanged(): return lax.all_to_all(values, 'tp', split_axis=0, concat_axis=0, tiled=True)  46.4 us
    ppermute x5, starting transfers between devices, swapped(): lax.ppermute(values, axis, [(i, i ^ bit) for i in range(lax.axis_size(axi...  29.5 us
    ppermute x2, waiting for transfers between devices, moved_down(): lax.ppermute(values, 'section', [(i, i - 1) for i in range(1, lax.axis_si...  8.18 us
    pallas_call x8, Pallas kernels, call(): pl.pallas_call(kernel, out_shape=outs, cost_estimate=cost(flops, outs, ar...  7.37 us
    unnamed x14, local copies, waits for them, and re-layouts  4.3 us
    ppermute x2, starting transfers between devices, moved_down(): lax.ppermute(values, 'section', [(i, i - 1) for i in range(1, lax.axis_si...  2.58 us
    pallas_call x2, Pallas kernels, prepared(): pl.pallas_call(kernel, grid_spec=pltpu.PrefetchScalarGridSpec(num_scalar_...  2.12 us
  transfers between devices with their start and end apart: 7, of which 4 were waited for; matrix products, arithmetic and copies ran while one was open for 0% of the time, Pallas kernels for 5%

profile of v3, /device:TPU:1, one launch (start us, length us, event | category | flops | bytes accessed | tf_op | source)
XLA Modules:
  0.0 104.5 jit_solution(1149810438124806914)
XLA Ops:
  0.6 4.0 %collective-permute-start = (bf16[576,512]{1,0:T(8,128)(2,1)}, bf16[576,512]{1,0:T(8,128)(2,1)S(1)}, u32[]{:S(2)}, u32[]{:S(2)}) collective-permute-start(bf16[576,512]{1,0:T(8,128)(2,1)} %bitcast.3), channel_id=1, source_target_pairs={{0,8},{4,12},{8,0},{12,4},{1,9},{5,13},{9,1},{13,5},{2,10},{6,14},... | collective-permute-start | bytes 1769480 | tf_op jit(solution)/shard_map/ppermute | solution.py:220
  4.7 13.9 %collective-permute-start.1 = (bf16[576,512]{1,0:T(8,128)(2,1)}, bf16[576,512]{1,0:T(8,128)(2,1)S(1)}, u32[]{:S(2)}, u32[]{:S(2)}) collective-permute-start(bf16[576,512]{1,0:T(8,128)(2,1)} %bitcast.4), channel_id=1, source_target_pairs={{0,4},{4,0},{8,12},{12,8},{1,5},{5,1},{9,13},{13,9},{2,6},{6,2},{1... | collective-permute-start | bytes 1769480 | tf_op jit(solution)/shard_map/ppermute | solution.py:220
  18.6 0.0 copy-start.1
  18.6 1.7 %copy-done.1 = bf16[1,4,128,2304]{3,2,1,0:T(8,128)(2,1)S(1)} copy-done((bf16[1,4,128,2304]{3,2,1,0:T(8,128)(2,1)S(1)}, bf16[1,4,128,2304]{3,2,1,0:T(8,128)(2,1)}, u32[]{:S(2)}) %copy-start.1) | copy-done | bytes 2359320
  20.3 0.0 copy-start.2
  20.3 1.3 %copy-done.2 = bf16[2,128,2304]{2,1,0:T(8,128)(2,1)S(1)} copy-done((bf16[2,128,2304]{2,1,0:T(8,128)(2,1)S(1)}, bf16[2,128,2304]{2,1,0:T(8,128)(2,1)}, u32[]{:S(2)}) %copy-start.2) | copy-done | bytes 1179672
  21.5 0.0 copy-start.5
  21.5 0.7 copy-done.5
  22.2 0.0 copy-start.6
  22.2 0.7 copy-done.6
  22.9 0.0 copy-start.4
  22.9 1.1 %shard_map.78 = (bf16[4,128,576]{2,1,0:T(8,128)(2,1)S(1)}, bf16[128,576]{1,0:T(8,128)(2,1)S(1)}, f32[128,128]{1,0:T(8,128)S(1)}, bf16[4,128,576]{2,1,0:T(8,128)(2,1)S(1)}) custom-call(s32[1,4]{1,0:T(1,128)S(1)} %copy-done.6, bf16[1,4,128,2304]{3,2,1,0:T(8,128)(2,1)S(1)} %copy-done.1, f32[1,2304]{1,0:T(1,128)S(1)} %copy-done.5, ...), custom_call_target="tpu_custom_call" | custom-call | flops 301989888 | bytes 1401856 | tf_op jit(solution)/shard_map/pallas_call | solution.py:259
  24.0 0.0 copy-done.4
  24.0 0.0 copy-start
  24.0 1.1 %shard_map.77 = (bf16[4,256,576]{2,1,0:T(8,128)(2,1)S(1)}, bf16[128,576]{1,0:T(8,128)(2,1)S(1)}, f32[128,128]{1,0:T(8,128)S(1)}, bf16[128,576]{1,0:T(8,128)(2,1)S(1)}, f32[1,576]{1,0:T(1,128)S(1)}) custom-call(s32[1,4]{1,0:T(1,128)S(1)} %copy-done.6, bf16[1,4,128,2304]{3,2,1,0:T(8,128)(2,1)S(1)} %copy-done.1, f32[1,2304]{1,0:T(1,128)S(1)} %copy-done.5, ...), custom_call_target="tpu_custom_call" | custom-call | flops 301989888 | bytes 1551616 | tf_op jit(solution)/shard_map/pallas_call | solution.py:259
  25.0 0.0 collective-permute-done.w2
  25.1 3.6 %collective-permute-start.2 = (bf16[576,512]{1,0:T(8,128)(2,1)S(1)}, bf16[576,512]{1,0:T(8,128)(2,1)S(1)}, u32[]{:S(2)}, u32[]{:S(2)}) collective-permute-start(bf16[576,512]{1,0:T(8,128)(2,1)S(1)} %collective-permute-done.w2), channel_id=1, source_target_pairs={{0,4},{4,0},{8,12},{12,8},{1,5},{5,1},{9,13},{13,9},{2,6},{6,2},{1... | collective-permute-start | bytes 1769480 | tf_op jit(solution)/shard_map/ppermute | solution.py:220
  28.6 0.0 collective-permute-done.1.w1
  28.6 0.0 copy-done
  28.7 0.8 shard_map.79.part_ref
  29.4 0.8 collective-permute-done.2.w3
  30.2 1.3 %shard_map.80 = (bf16[256,512]{1,0:T(8,128)(2,1)S(1)}, bf16[4,128,640]{2,1,0:T(8,128)(2,1)S(1)}) custom-call(f32[256,512]{1,0:T(8,128)S(1)} %shard_map.79.part_ref, bf16[4,256,576]{2,1,0:T(8,128)(2,1)S(1)} %get-tuple-element.50.left_ref, bf16[576,512]{1,0:T(8,128)(2,1)S(1)} %bitcast.6, bf16[576,512]{1,0:T(8,128)(2,1)S(1)} %collective-permute-done.1.w1, ...), custom_call_target="tpu_custom_call" | custom-call | flops 603979776 | bytes 4980736 | tf_op jit(solution)/shard_map/pallas_call | solution.py:47
  31.6 13.0 %all_to_all.20.got_ref = bf16[4,128,640]{2,1,0:T(8,128)(2,1)S(1)} all-to-all(bf16[4,128,640]{2,1,0:T(8,128)(2,1)S(1)} %get-tuple-element.52), channel_id=1, replica_groups=mesh['section'=64,'fsdp'=4,'tp'=4] {'tp'}, dimensions={0} | all-to-all | bytes 1310720 | tf_op jit(solution)/shard_map/all_to_all | solution.py:230
  44.6 0.3 shard_map.81
  44.9 1.3 %collective-permute-start.3 = (bf16[64,1152]{1,0:T(8,128)(2,1)S(1)}, bf16[64,1152]{1,0:T(8,128)(2,1)S(1)}, u32[]{:S(2)}, u32[]{:S(2)}) collective-permute-start(bf16[64,1152]{1,0:T(8,128)(2,1)S(1)} %shard_map.81), channel_id=1, source_target_pairs={{16,0},{32,16},{48,32},{64,48},{80,64},{96,80},{112,96},{128,112},... | collective-permute-start | bytes 442376 | tf_op jit(solution)/shard_map/ppermute | solution.py:224
  46.2 1.3 %shard_map.82 = (f32[4,576,512]{2,1,0:T(8,128)S(1)}, bf16[128,512]{1,0:T(8,128)(2,1)S(1)}, f32[128,512]{1,0:T(8,128)S(1)}, f32[128,512]{1,0:T(8,128)S(1)}) custom-call(bf16[4,256,576]{2,1,0:T(8,128)(2,1)S(1)} %get-tuple-element.50.left_ref, bf16[256,512]{1,0:T(8,128)(2,1)S(1)} %get-tuple-element.57.right_ref, ...), custom_call_target="tpu_custom_call" | custom-call | flops 905969664 | bytes 9764864 | tf_op jit(solution)/shard_map/pallas_call | solution.py:47
  47.5 4.8 %collective-permute-done.3 = bf16[64,1152]{1,0:T(8,128)(2,1)S(1)} collective-permute-done((bf16[64,1152]{1,0:T(8,128)(2,1)S(1)}, bf16[64,1152]{1,0:T(8,128)(2,1)S(1)}, u32[]{:S(2)}, u32[]{:S(2)}) %collective-permute-start.3) | collective-permute-done | bytes 147488 | tf_op jit(solution)/shard_map/ppermute | solution.py:224
  52.3 10.0 %all_to_all.21.got_ref = bf16[4,64,1152]{2,1,0:T(8,128)(2,1)S(1)} all-to-all(bf16[4,64,1152]{2,1,0:T(8,128)(2,1)S(1)} %broadcast_in_dim.6), channel_id=1, replica_groups=mesh['section'=64,'fsdp'=4,'tp'=4] {'tp'}, dimensions={0} | all-to-all | bytes 1179648 | tf_op jit(solution)/shard_map/all_to_all | solution.py:230
  62.3 1.6 %shard_map.83 = (bf16[4,128,576]{2,1,0:T(8,128)(2,1)S(1)}, bf16[128,512]{1,0:T(8,128)(2,1)S(1)}, bf16[4,128,640]{2,1,0:T(8,128)(2,1)S(1)}, bf16[128,576]{1,0:T(8,128)(2,1)S(1)}) custom-call(f32[128,512]{1,0:T(8,128)S(1)} %get-tuple-element.63.hidden_ref, f32[128,512]{1,0:T(8,128)S(1)} %get-tuple-element.64.slope_ref, ...), custom_call_target="tpu_custom_call" | custom-call | flops 603979776 | bytes 5586944 | tf_op jit(solution)/shard_map/pallas_call | solution.py:47
  63.9 0.8 shard_map.84
  64.8 5.4 %collective-permute-start.5 = (bf16[2,576,512]{2,1,0:T(8,128)(2,1)S(1)}, bf16[2,576,512]{2,1,0:T(8,128)(2,1)S(1)}, u32[]{:S(2)}, u32[]{:S(2)}) collective-permute-start(bf16[2,576,512]{2,1,0:T(8,128)(2,1)S(1)} %get-tuple-element.79), channel_id=1, source_target_pairs={{0,4},{4,0},{8,12},{12,8},{1,5},{5,1},{9,13},{13,9},{2,6},{6,2},{1... | collective-permute-start | bytes 3538952 | tf_op jit(solution)/shard_map/ppermute | solution.py:220
  70.2 13.1 %all_to_all.22.got_ref = bf16[4,128,640]{2,1,0:T(8,128)(2,1)S(1)} all-to-all(bf16[4,128,640]{2,1,0:T(8,128)(2,1)S(1)} %get-tuple-element.74), channel_id=1, replica_groups=mesh['section'=64,'fsdp'=4,'tp'=4] {'tp'}, dimensions={0} | all-to-all | bytes 1310720 | tf_op jit(solution)/shard_map/all_to_all | solution.py:230
  83.3 0.3 shard_map.85
  83.6 1.3 %collective-permute-start.4 = (bf16[64,1152]{1,0:T(8,128)(2,1)S(1)}, bf16[64,1152]{1,0:T(8,128)(2,1)S(1)}, u32[]{:S(2)}, u32[]{:S(2)}) collective-permute-start(bf16[64,1152]{1,0:T(8,128)(2,1)S(1)} %shard_map.85), channel_id=1, source_target_pairs={{16,0},{32,16},{48,32},{64,48},{80,64},{96,80},{112,96},{128,112},... | collective-permute-start | bytes 442376 | tf_op jit(solution)/shard_map/ppermute | solution.py:224
  84.9 0.0 collective-permute-done.5.core_ref
  84.9 0.2 fusion
  85.1 0.0 copy-start.3
  85.1 2.5 %collective-permute-start.6 = (bf16[576,512]{1,0:T(8,128)(2,1)S(1)}, bf16[576,512]{1,0:T(8,128)(2,1)S(1)}, u32[]{:S(2)}, u32[]{:S(2)}) collective-permute-start(bf16[576,512]{1,0:T(8,128)(2,1)S(1)} %fusion), channel_id=1, source_target_pairs={{0,8},{4,12},{8,0},{12,4},{1,9},{5,13},{9,1},{13,5},{2,10},{6,14},... | collective-permute-start | bytes 1769480 | tf_op jit(solution)/shard_map/ppermute | solution.py:220
  87.6 3.4 %collective-permute-done.4 = bf16[64,1152]{1,0:T(8,128)(2,1)S(1)} collective-permute-done((bf16[64,1152]{1,0:T(8,128)(2,1)S(1)}, bf16[64,1152]{1,0:T(8,128)(2,1)S(1)}, u32[]{:S(2)}, u32[]{:S(2)}) %collective-permute-start.4) | collective-permute-done | bytes 147488 | tf_op jit(solution)/shard_map/ppermute | solution.py:224
  91.0 10.3 %all_to_all.23.got_ref = bf16[4,64,1152]{2,1,0:T(8,128)(2,1)S(1)} all-to-all(bf16[4,64,1152]{2,1,0:T(8,128)(2,1)S(1)} %broadcast_in_dim.7), channel_id=1, replica_groups=mesh['section'=64,'fsdp'=4,'tp'=4] {'tp'}, dimensions={0} | all-to-all | bytes 1179648 | tf_op jit(solution)/shard_map/all_to_all | solution.py:230
  101.4 0.0 copy-done.3
  101.4 1.0 shard_map.86
  102.4 0.6 collective-permute-done.6.across_ref
  102.9 1.6 %shard_map.87 = f32[1,576,512]{2,1,0:T(8,128)} custom-call(f32[2,576,512]{2,1,0:T(8,128)S(1)} %get-tuple-element.78.keep_ref, bf16[2,576,512]{2,1,0:T(8,128)(2,1)S(1)} %collective-permute-done.5.core_ref, bf16[576,512]{1,0:T(8,128)(2,1)S(1)} %collective-permute-done.6.across_ref), custom_call_target="tpu_custom_call" | custom-call | tf_op jit(solution)/shard_map/pallas_call | solution.py:333
  (2 shorter events, 0.1 us)
Async XLA Ops:
  0.6 24.4 %collective-permute-start = (bf16[576,512]{1,0:T(8,128)(2,1)}, bf16[576,512]{1,0:T(8,128)(2,1)S(1)}, u32[]{:S(2)}, u32[]{:S(2)}) collective-permute-start(bf16[576,512]{1,0:T(8,128)(2,1)} %bitcast.3), channel_id=1, source_target_pairs={{0,8},{4,12},{8,0},{12,4},{1,9},{5,13},{9,1},{13,5},{2,10},{6,14},... | collective-permute-start | bytes 1769480 | tf_op jit(solution)/shard_map/ppermute | solution.py:220
  4.7 24.0 %collective-permute-start.1 = (bf16[576,512]{1,0:T(8,128)(2,1)}, bf16[576,512]{1,0:T(8,128)(2,1)S(1)}, u32[]{:S(2)}, u32[]{:S(2)}) collective-permute-start(bf16[576,512]{1,0:T(8,128)(2,1)} %bitcast.4), channel_id=1, source_target_pairs={{0,4},{4,0},{8,12},{12,8},{1,5},{5,1},{9,13},{13,9},{2,6},{6,2},{1... | collective-permute-start | bytes 1769480 | tf_op jit(solution)/shard_map/ppermute | solution.py:220
  18.6 1.7 %copy-start.1 = (bf16[1,4,128,2304]{3,2,1,0:T(8,128)(2,1)S(1)}, bf16[1,4,128,2304]{3,2,1,0:T(8,128)(2,1)}, u32[]{:S(2)}) copy-start(bf16[1,4,128,2304]{3,2,1,0:T(8,128)(2,1)} %stash_ref.3) | copy-start | bytes 7077892
  20.3 1.3 %copy-start.2 = (bf16[2,128,2304]{2,1,0:T(8,128)(2,1)S(1)}, bf16[2,128,2304]{2,1,0:T(8,128)(2,1)}, u32[]{:S(2)}) copy-start(bf16[2,128,2304]{2,1,0:T(8,128)(2,1)} %top_ref.3) | copy-start | bytes 3538948
  21.5 0.7 copy-start.5
  22.2 0.7 copy-start.6
  22.9 1.1 %copy-start.4 = (bf16[1,128,2304]{2,1,0:T(8,128)(2,1)S(1)}, bf16[1,128,2304]{2,1,0:T(8,128)(2,1)}, u32[]{:S(2)}) copy-start(bf16[1,128,2304]{2,1,0:T(8,128)(2,1)} %now_ref.1) | copy-start | bytes 1769476
  24.0 4.7 %copy-start = (bf16[1,576,512]{2,1,0:T(8,128)(2,1)S(1)}, bf16[1,576,512]{2,1,0:T(8,128)(2,1)}, u32[]{:S(2)}) copy-start(bf16[1,576,512]{2,1,0:T(8,128)(2,1)} %param.11) | copy-start | bytes 1769476
  25.1 5.2 %collective-permute-start.2 = (bf16[576,512]{1,0:T(8,128)(2,1)S(1)}, bf16[576,512]{1,0:T(8,128)(2,1)S(1)}, u32[]{:S(2)}, u32[]{:S(2)}) collective-permute-start(bf16[576,512]{1,0:T(8,128)(2,1)S(1)} %collective-permute-done.w2), channel_id=1, source_target_pairs={{0,4},{4,0},{8,12},{12,8},{1,5},{5,1},{9,13},{13,9},{2,6},{6,2},{1... | collective-permute-start | bytes 1769480 | tf_op jit(solution)/shard_map/ppermute | solution.py:220
  44.9 7.4 %collective-permute-start.3 = (bf16[64,1152]{1,0:T(8,128)(2,1)S(1)}, bf16[64,1152]{1,0:T(8,128)(2,1)S(1)}, u32[]{:S(2)}, u32[]{:S(2)}) collective-permute-start(bf16[64,1152]{1,0:T(8,128)(2,1)S(1)} %shard_map.81), channel_id=1, source_target_pairs={{16,0},{32,16},{48,32},{64,48},{80,64},{96,80},{112,96},{128,112},... | collective-permute-start | bytes 442376 | tf_op jit(solution)/shard_map/ppermute | solution.py:224
  64.8 20.1 %collective-permute-start.5 = (bf16[2,576,512]{2,1,0:T(8,128)(2,1)S(1)}, bf16[2,576,512]{2,1,0:T(8,128)(2,1)S(1)}, u32[]{:S(2)}, u32[]{:S(2)}) collective-permute-start(bf16[2,576,512]{2,1,0:T(8,128)(2,1)S(1)} %get-tuple-element.79), channel_id=1, source_target_pairs={{0,4},{4,0},{8,12},{12,8},{1,5},{5,1},{9,13},{13,9},{2,6},{6,2},{1... | collective-permute-start | bytes 3538952 | tf_op jit(solution)/shard_map/ppermute | solution.py:220
  83.6 7.4 %collective-permute-start.4 = (bf16[64,1152]{1,0:T(8,128)(2,1)S(1)}, bf16[64,1152]{1,0:T(8,128)(2,1)S(1)}, u32[]{:S(2)}, u32[]{:S(2)}) collective-permute-start(bf16[64,1152]{1,0:T(8,128)(2,1)S(1)} %shard_map.85), channel_id=1, source_target_pairs={{16,0},{32,16},{48,32},{64,48},{80,64},{96,80},{112,96},{128,112},... | collective-permute-start | bytes 442376 | tf_op jit(solution)/shard_map/ppermute | solution.py:224
  85.1 16.3 %copy-start.3 = (bf16[2,128,2304]{2,1,0:T(8,128)(2,1)S(1)}, bf16[2,128,2304]{2,1,0:T(8,128)(2,1)}, u32[]{:S(2)}) copy-start(bf16[2,128,2304]{2,1,0:T(8,128)(2,1)} %top_ref.3) | copy-start | bytes 3538948
  85.1 17.8 %collective-permute-start.6 = (bf16[576,512]{1,0:T(8,128)(2,1)S(1)}, bf16[576,512]{1,0:T(8,128)(2,1)S(1)}, u32[]{:S(2)}, u32[]{:S(2)}) collective-permute-start(bf16[576,512]{1,0:T(8,128)(2,1)S(1)} %fusion), channel_id=1, source_target_pairs={{0,8},{4,12},{8,0},{12,4},{1,9},{5,13},{9,1},{13,5},{2,10},{6,14},... | collective-permute-start | bytes 1769480 | tf_op jit(solution)/shard_map/ppermute | solution.py:220

commit v4 on v3

--- a/solution.py
+++ b/solution.py
@@ -210,10 +210,6 @@
         for b in range(count):
             held_ref[0, :rows, b * width : (b + 1) * width] = got_ref[b, :, :width]
             held_ref[0, rows:, b * width : (b + 1) * width] = got_ref[b, :, width:]
-
-
-def join_kernel(keep_ref, core_ref, across_ref, grad_ref):
-    grad_ref[0] = keep_ref[0] + core_ref[0].astype(f32) + across_ref[...].astype(f32)
 
 
 def swapped(values, axis, bit):
@@ -312,6 +308,9 @@
         [blocks, flat, sent, own],
         hidden2, slope2, held1, top1, *weights,
     )
+    got2 = exchanged(out2)
+    share2 = call(own_share, dot // 8, share, got2, x2, inv2, gains, dy2_own)
+    arrived2 = moved_down(share2)
     pair = (tp_count // 2, width, inner)
     keep, send = call(
         late_kernel,
@@ -319,30 +318,13 @@
         [sds(pair, f32), sds(pair, bf16)],
         h2, dy2, pre2, act2, acc,
     )
-    (out2, keep, send) = lax.optimization_barrier((out2, keep, send))
-    got2 = exchanged(out2)
-    share2 = call(own_share, dot // 8, share, got2, x2, inv2, gains, dy2_own)
-    arrived2 = moved_down(share2)
     from_core = swapped(send, "fsdp", 1)
     across = keep[1] + from_core[1].astype(f32)
     across = swapped(across.astype(bf16), "fsdp", 2)
     held2 = copied_to_all(arrived2)
     grad_held = call(last_kernel, dot // 8, sds((1, tokens, features), bf16), held2, grad_top)
-    steps = 3
-    grad_rows = width // steps
-    weight_grad = pl.pallas_call(
-        join_kernel,
-        grid=(steps,),
-        in_specs=[
-            pl.BlockSpec((1, grad_rows, inner), lambda i: (0, i, 0)),
-            pl.BlockSpec((1, grad_rows, inner), lambda i: (0, i, 0)),
-            pl.BlockSpec((grad_rows, inner), lambda i: (i, 0)),
-        ],
-        out_specs=pl.BlockSpec((1, grad_rows, inner), lambda i: (0, i, 0)),
-        out_shape=sds((1, width, inner), f32),
-        compiler_params=pltpu.CompilerParams(vmem_limit_bytes=vmem_budget),
-    )(keep, from_core, across)
-    return (grad_held, weight_grad)
+    weight_grad = keep[0] + from_core[0].astype(f32) + across.astype(f32)
+    return (grad_held, weight_grad[None])
 
 
 def solution(mesh):

time: 106 us -> 105 us (level)
  Pallas kernels: 11.1 us -> 9.5 us
  other arithmetic: 0.19 us -> 1.42 us
    pallas_call x1 -> x0, Pallas kernels: 1.6 us -> none  [per_device(): pl.pallas_call(join_kernel, grid=(steps,), in_specs=[pl.BlockSpec((1, gra...]
    broadcast_in_dim x0 -> x1, other arithmetic: none -> 1.24 us  [per_device(): return (grad_held, weight_grad[None])]
where the time goes in v4:
time: 105 us; the launch traced here: 104 us
  blocking collectives  46.4 us (44%)
  starting transfers between devices  32 us (30%)
  waiting for transfers between devices  9.55 us (9%)
  Pallas kernels  9.5 us (9%)
  local copies, waits for them, and re-layouts  4.38 us (4%)
  other arithmetic  1.42 us (1%)
    all_to_all x4, blocking collectives, exchanged(): return lax.all_to_all(values, 'tp', split_axis=0, concat_axis=0, tiled=True)  46.4 us
    ppermute x5, starting transfers between devices, swapped(): lax.ppermute(values, axis, [(i, i ^ bit) for i in range(lax.axis_size(axi...  29.5 us
    ppermute x2, waiting for transfers between devices, moved_down(): lax.ppermute(values, 'section', [(i, i - 1) for i in range(1, lax.axis_si...  8.18 us
    pallas_call x8, Pallas kernels, call(): pl.pallas_call(kernel, out_shape=outs, cost_estimate=cost(flops, outs, ar...  7.37 us
    unnamed x14, local copies, waits for them, and re-layouts  4.3 us
    ppermute x2, starting transfers between devices, moved_down(): lax.ppermute(values, 'section', [(i, i - 1) for i in range(1, lax.axis_si...  2.58 us
    pallas_call x2, Pallas kernels, prepared(): pl.pallas_call(kernel, grid_spec=pltpu.PrefetchScalarGridSpec(num_scalar_...  2.12 us
  transfers between devices with their start and end apart: 7, of which 4 were waited for; matrix products, arithmetic and copies ran while one was open for 0% of the time, Pallas kernels for 5%

profile of v4, /device:TPU:1, one launch (start us, length us, event | category | flops | bytes accessed | tf_op | source)
XLA Modules:
  0.0 104.2 jit_solution(2997608657803384431)
XLA Ops:
  0.6 4.0 %collective-permute-start = (bf16[576,512]{1,0:T(8,128)(2,1)}, bf16[576,512]{1,0:T(8,128)(2,1)S(1)}, u32[]{:S(2)}, u32[]{:S(2)}) collective-permute-start(bf16[576,512]{1,0:T(8,128)(2,1)} %bitcast.9), channel_id=1, source_target_pairs={{0,8},{4,12},{8,0},{12,4},{1,9},{5,13},{9,1},{13,5},{2,10},{6,14},... | collective-permute-start | bytes 1769480 | tf_op jit(solution)/shard_map/ppermute | solution.py:216
  4.7 13.9 %collective-permute-start.1 = (bf16[576,512]{1,0:T(8,128)(2,1)}, bf16[576,512]{1,0:T(8,128)(2,1)S(1)}, u32[]{:S(2)}, u32[]{:S(2)}) collective-permute-start(bf16[576,512]{1,0:T(8,128)(2,1)} %bitcast.10), channel_id=1, source_target_pairs={{0,4},{4,0},{8,12},{12,8},{1,5},{5,1},{9,13},{13,9},{2,6},{6,2},{1... | collective-permute-start | bytes 1769480 | tf_op jit(solution)/shard_map/ppermute | solution.py:216
  18.6 0.0 copy-start.1
  18.6 1.7 %copy-done.1 = bf16[1,4,128,2304]{3,2,1,0:T(8,128)(2,1)S(1)} copy-done((bf16[1,4,128,2304]{3,2,1,0:T(8,128)(2,1)S(1)}, bf16[1,4,128,2304]{3,2,1,0:T(8,128)(2,1)}, u32[]{:S(2)}) %copy-start.1) | copy-done | bytes 2359320
  20.3 0.0 copy-start.2
  20.3 1.3 %copy-done.2 = bf16[2,128,2304]{2,1,0:T(8,128)(2,1)S(1)} copy-done((bf16[2,128,2304]{2,1,0:T(8,128)(2,1)S(1)}, bf16[2,128,2304]{2,1,0:T(8,128)(2,1)}, u32[]{:S(2)}) %copy-start.2) | copy-done | bytes 1179672
  21.5 0.0 copy-start.5
  21.5 0.7 copy-done.5
  22.2 0.0 copy-start.6
  22.2 0.7 copy-done.6
  22.9 0.0 copy-start.4
  22.9 1.1 %shard_map.78 = (bf16[4,128,576]{2,1,0:T(8,128)(2,1)S(1)}, bf16[128,576]{1,0:T(8,128)(2,1)S(1)}, f32[128,128]{1,0:T(8,128)S(1)}, bf16[4,128,576]{2,1,0:T(8,128)(2,1)S(1)}) custom-call(s32[1,4]{1,0:T(1,128)S(1)} %copy-done.6, bf16[1,4,128,2304]{3,2,1,0:T(8,128)(2,1)S(1)} %copy-done.1, f32[1,2304]{1,0:T(1,128)S(1)} %copy-done.5, ...), custom_call_target="tpu_custom_call" | custom-call | flops 301989888 | bytes 1401856 | tf_op jit(solution)/shard_map/pallas_call | solution.py:255
  24.0 0.0 copy-done.4
  24.0 0.0 copy-start
  24.0 1.1 %shard_map.77 = (bf16[4,256,576]{2,1,0:T(8,128)(2,1)S(1)}, bf16[128,576]{1,0:T(8,128)(2,1)S(1)}, f32[128,128]{1,0:T(8,128)S(1)}, bf16[128,576]{1,0:T(8,128)(2,1)S(1)}, f32[1,576]{1,0:T(1,128)S(1)}) custom-call(s32[1,4]{1,0:T(1,128)S(1)} %copy-done.6, bf16[1,4,128,2304]{3,2,1,0:T(8,128)(2,1)S(1)} %copy-done.1, f32[1,2304]{1,0:T(1,128)S(1)} %copy-done.5, ...), custom_call_target="tpu_custom_call" | custom-call | flops 301989888 | bytes 1551616 | tf_op jit(solution)/shard_map/pallas_call | solution.py:255
  25.0 0.0 collective-permute-done.w2
  25.1 3.6 %collective-permute-start.2 = (bf16[576,512]{1,0:T(8,128)(2,1)S(1)}, bf16[576,512]{1,0:T(8,128)(2,1)S(1)}, u32[]{:S(2)}, u32[]{:S(2)}) collective-permute-start(bf16[576,512]{1,0:T(8,128)(2,1)S(1)} %collective-permute-done.w2), channel_id=1, source_target_pairs={{0,4},{4,0},{8,12},{12,8},{1,5},{5,1},{9,13},{13,9},{2,6},{6,2},{1... | collective-permute-start | bytes 1769480 | tf_op jit(solution)/shard_map/ppermute | solution.py:216
  28.6 0.0 collective-permute-done.1.w1
  28.6 0.0 copy-done
  28.7 0.8 shard_map.79.part_ref
  29.4 0.8 collective-permute-done.2.w3
  30.2 1.3 %shard_map.80 = (bf16[256,512]{1,0:T(8,128)(2,1)S(1)}, bf16[4,128,640]{2,1,0:T(8,128)(2,1)S(1)}) custom-call(f32[256,512]{1,0:T(8,128)S(1)} %shard_map.79.part_ref, bf16[4,256,576]{2,1,0:T(8,128)(2,1)S(1)} %get-tuple-element.47.left_ref, bf16[576,512]{1,0:T(8,128)(2,1)S(1)} %bitcast.12, bf16[576,512]{1,0:T(8,128)(2,1)S(1)} %collective-permute-done.1.w1, ...), custom_call_target="tpu_custom_call" | custom-call | flops 603979776 | bytes 4980736 | tf_op jit(solution)/shard_map/pallas_call | solution.py:47
  31.6 13.0 %all_to_all.20.got_ref = bf16[4,128,640]{2,1,0:T(8,128)(2,1)S(1)} all-to-all(bf16[4,128,640]{2,1,0:T(8,128)(2,1)S(1)} %get-tuple-element.49), channel_id=1, replica_groups=mesh['section'=64,'fsdp'=4,'tp'=4] {'tp'}, dimensions={0} | all-to-all | bytes 1310720 | tf_op jit(solution)/shard_map/all_to_all | solution.py:226
  44.6 0.3 shard_map.81
  44.9 1.3 %collective-permute-start.3 = (bf16[64,1152]{1,0:T(8,128)(2,1)S(1)}, bf16[64,1152]{1,0:T(8,128)(2,1)S(1)}, u32[]{:S(2)}, u32[]{:S(2)}) collective-permute-start(bf16[64,1152]{1,0:T(8,128)(2,1)S(1)} %shard_map.81), channel_id=1, source_target_pairs={{16,0},{32,16},{48,32},{64,48},{80,64},{96,80},{112,96},{128,112},... | collective-permute-start | bytes 442376 | tf_op jit(solution)/shard_map/ppermute | solution.py:220
  46.2 1.3 %shard_map.82 = (f32[4,576,512]{2,1,0:T(8,128)S(1)}, bf16[128,512]{1,0:T(8,128)(2,1)S(1)}, f32[128,512]{1,0:T(8,128)S(1)}, f32[128,512]{1,0:T(8,128)S(1)}) custom-call(bf16[4,256,576]{2,1,0:T(8,128)(2,1)S(1)} %get-tuple-element.47.left_ref, bf16[256,512]{1,0:T(8,128)(2,1)S(1)} %get-tuple-element.54.right_ref, ...), custom_call_target="tpu_custom_call" | custom-call | flops 905969664 | bytes 9764864 | tf_op jit(solution)/shard_map/pallas_call | solution.py:47
  47.5 4.8 %collective-permute-done.3 = bf16[64,1152]{1,0:T(8,128)(2,1)S(1)} collective-permute-done((bf16[64,1152]{1,0:T(8,128)(2,1)S(1)}, bf16[64,1152]{1,0:T(8,128)(2,1)S(1)}, u32[]{:S(2)}, u32[]{:S(2)}) %collective-permute-start.3) | collective-permute-done | bytes 147488 | tf_op jit(solution)/shard_map/ppermute | solution.py:220
  52.3 10.0 %all_to_all.21.got_ref = bf16[4,64,1152]{2,1,0:T(8,128)(2,1)S(1)} all-to-all(bf16[4,64,1152]{2,1,0:T(8,128)(2,1)S(1)} %broadcast_in_dim.9), channel_id=1, replica_groups=mesh['section'=64,'fsdp'=4,'tp'=4] {'tp'}, dimensions={0} | all-to-all | bytes 1179648 | tf_op jit(solution)/shard_map/all_to_all | solution.py:226
  62.3 1.6 %shard_map.83 = (bf16[4,128,576]{2,1,0:T(8,128)(2,1)S(1)}, bf16[128,512]{1,0:T(8,128)(2,1)S(1)}, bf16[4,128,640]{2,1,0:T(8,128)(2,1)S(1)}, bf16[128,576]{1,0:T(8,128)(2,1)S(1)}) custom-call(f32[128,512]{1,0:T(8,128)S(1)} %get-tuple-element.60.hidden_ref, f32[128,512]{1,0:T(8,128)S(1)} %get-tuple-element.61.slope_ref, ...), custom_call_target="tpu_custom_call" | custom-call | flops 603979776 | bytes 5586944 | tf_op jit(solution)/shard_map/pallas_call | solution.py:47
  63.9 0.8 shard_map.86
  64.8 5.4 %collective-permute-start.5 = (bf16[2,576,512]{2,1,0:T(8,128)(2,1)S(1)}, bf16[2,576,512]{2,1,0:T(8,128)(2,1)S(1)}, u32[]{:S(2)}, u32[]{:S(2)}) collective-permute-start(bf16[2,576,512]{2,1,0:T(8,128)(2,1)S(1)} %get-tuple-element.73), channel_id=1, source_target_pairs={{0,4},{4,0},{8,12},{12,8},{1,5},{5,1},{9,13},{13,9},{2,6},{6,2},{1... | collective-permute-start | bytes 3538952 | tf_op jit(solution)/shard_map/ppermute | solution.py:216
  70.2 13.1 %all_to_all.22.got_ref = bf16[4,128,640]{2,1,0:T(8,128)(2,1)S(1)} all-to-all(bf16[4,128,640]{2,1,0:T(8,128)(2,1)S(1)} %get-tuple-element.64), channel_id=1, replica_groups=mesh['section'=64,'fsdp'=4,'tp'=4] {'tp'}, dimensions={0} | all-to-all | bytes 1310720 | tf_op jit(solution)/shard_map/all_to_all | solution.py:226
  83.3 0.3 shard_map.84
  83.6 1.3 %collective-permute-start.4 = (bf16[64,1152]{1,0:T(8,128)(2,1)S(1)}, bf16[64,1152]{1,0:T(8,128)(2,1)S(1)}, u32[]{:S(2)}, u32[]{:S(2)}) collective-permute-start(bf16[64,1152]{1,0:T(8,128)(2,1)S(1)} %shard_map.84), channel_id=1, source_target_pairs={{16,0},{32,16},{48,32},{64,48},{80,64},{96,80},{112,96},{128,112},... | collective-permute-start | bytes 442376 | tf_op jit(solution)/shard_map/ppermute | solution.py:220
  84.9 0.0 collective-permute-done.5
  84.9 0.2 fusion.1
  85.1 0.0 copy-start.3
  85.1 2.5 %collective-permute-start.6 = (bf16[576,512]{1,0:T(8,128)(2,1)S(1)}, bf16[576,512]{1,0:T(8,128)(2,1)S(1)}, u32[]{:S(2)}, u32[]{:S(2)}) collective-permute-start(bf16[576,512]{1,0:T(8,128)(2,1)S(1)} %fusion.1), channel_id=1, source_target_pairs={{0,8},{4,12},{8,0},{12,4},{1,9},{5,13},{9,1},{13,5},{2,10},{6,14},... | collective-permute-start | bytes 1769480 | tf_op jit(solution)/shard_map/ppermute | solution.py:216
  87.6 3.4 %collective-permute-done.4 = bf16[64,1152]{1,0:T(8,128)(2,1)S(1)} collective-permute-done((bf16[64,1152]{1,0:T(8,128)(2,1)S(1)}, bf16[64,1152]{1,0:T(8,128)(2,1)S(1)}, u32[]{:S(2)}, u32[]{:S(2)}) %collective-permute-start.4) | collective-permute-done | bytes 147488 | tf_op jit(solution)/shard_map/ppermute | solution.py:220
  91.0 10.3 %all_to_all.23.got_ref = bf16[4,64,1152]{2,1,0:T(8,128)(2,1)S(1)} all-to-all(bf16[4,64,1152]{2,1,0:T(8,128)(2,1)S(1)} %broadcast_in_dim.10), channel_id=1, replica_groups=mesh['section'=64,'fsdp'=4,'tp'=4] {'tp'}, dimensions={0} | all-to-all | bytes 1179648 | tf_op jit(solution)/shard_map/all_to_all | solution.py:226
  101.4 0.0 copy-done.3
  101.4 1.0 shard_map.85
  102.4 0.6 collective-permute-done.6
  102.9 1.2 %fusion = f32[1,576,512]{2,1,0:T(8,128)} fusion(bf16[576,512]{1,0:T(8,128)(2,1)S(1)} %collective-permute-done.6, f32[2,576,512]{2,1,0:T(8,128)S(1)} %get-tuple-element.72, bf16[2,576,512]{2,1,0:T(8,128)(2,1)S(1)} %collective-permute-done.5), kind=kLoop, calls=%fused_computation.1 | loop fusion | flops 1179648 | bytes 3538944 | tf_op jit(solution)/shard_map/broadcast_in_dim | solution.py:327
  (2 shorter events, 0.1 us)
Async XLA Ops:
  0.6 24.4 %collective-permute-start = (bf16[576,512]{1,0:T(8,128)(2,1)}, bf16[576,512]{1,0:T(8,128)(2,1)S(1)}, u32[]{:S(2)}, u32[]{:S(2)}) collective-permute-start(bf16[576,512]{1,0:T(8,128)(2,1)} %bitcast.9), channel_id=1, source_target_pairs={{0,8},{4,12},{8,0},{12,4},{1,9},{5,13},{9,1},{13,5},{2,10},{6,14},... | collective-permute-start | bytes 1769480 | tf_op jit(solution)/shard_map/ppermute | solution.py:216
  4.7 24.0 %collective-permute-start.1 = (bf16[576,512]{1,0:T(8,128)(2,1)}, bf16[576,512]{1,0:T(8,128)(2,1)S(1)}, u32[]{:S(2)}, u32[]{:S(2)}) collective-permute-start(bf16[576,512]{1,0:T(8,128)(2,1)} %bitcast.10), channel_id=1, source_target_pairs={{0,4},{4,0},{8,12},{12,8},{1,5},{5,1},{9,13},{13,9},{2,6},{6,2},{1... | collective-permute-start | bytes 1769480 | tf_op jit(solution)/shard_map/ppermute | solution.py:216
  18.6 1.7 %copy-start.1 = (bf16[1,4,128,2304]{3,2,1,0:T(8,128)(2,1)S(1)}, bf16[1,4,128,2304]{3,2,1,0:T(8,128)(2,1)}, u32[]{:S(2)}) copy-start(bf16[1,4,128,2304]{3,2,1,0:T(8,128)(2,1)} %stash_ref.3) | copy-start | bytes 7077892
  20.3 1.3 %copy-start.2 = (bf16[2,128,2304]{2,1,0:T(8,128)(2,1)S(1)}, bf16[2,128,2304]{2,1,0:T(8,128)(2,1)}, u32[]{:S(2)}) copy-start(bf16[2,128,2304]{2,1,0:T(8,128)(2,1)} %top_ref.3) | copy-start | bytes 3538948
  21.5 0.7 copy-start.5
  22.2 0.7 copy-start.6
  22.9 1.1 %copy-start.4 = (bf16[1,128,2304]{2,1,0:T(8,128)(2,1)S(1)}, bf16[1,128,2304]{2,1,0:T(8,128)(2,1)}, u32[]{:S(2)}) copy-start(bf16[1,128,2304]{2,1,0:T(8,128)(2,1)} %now_ref.1) | copy-start | bytes 1769476
  24.0 4.7 %copy-start = (bf16[1,576,512]{2,1,0:T(8,128)(2,1)S(1)}, bf16[1,576,512]{2,1,0:T(8,128)(2,1)}, u32[]{:S(2)}) copy-start(bf16[1,576,512]{2,1,0:T(8,128)(2,1)} %param.11) | copy-start | bytes 1769476
  25.1 5.2 %collective-permute-start.2 = (bf16[576,512]{1,0:T(8,128)(2,1)S(1)}, bf16[576,512]{1,0:T(8,128)(2,1)S(1)}, u32[]{:S(2)}, u32[]{:S(2)}) collective-permute-start(bf16[576,512]{1,0:T(8,128)(2,1)S(1)} %collective-permute-done.w2), channel_id=1, source_target_pairs={{0,4},{4,0},{8,12},{12,8},{1,5},{5,1},{9,13},{13,9},{2,6},{6,2},{1... | collective-permute-start | bytes 1769480 | tf_op jit(solution)/shard_map/ppermute | solution.py:216
  44.9 7.4 %collective-permute-start.3 = (bf16[64,1152]{1,0:T(8,128)(2,1)S(1)}, bf16[64,1152]{1,0:T(8,128)(2,1)S(1)}, u32[]{:S(2)}, u32[]{:S(2)}) collective-permute-start(bf16[64,1152]{1,0:T(8,128)(2,1)S(1)} %shard_map.81), channel_id=1, source_target_pairs={{16,0},{32,16},{48,32},{64,48},{80,64},{96,80},{112,96},{128,112},... | collective-permute-start | bytes 442376 | tf_op jit(solution)/shard_map/ppermute | solution.py:220
  64.8 20.1 %collective-permute-start.5 = (bf16[2,576,512]{2,1,0:T(8,128)(2,1)S(1)}, bf16[2,576,512]{2,1,0:T(8,128)(2,1)S(1)}, u32[]{:S(2)}, u32[]{:S(2)}) collective-permute-start(bf16[2,576,512]{2,1,0:T(8,128)(2,1)S(1)} %get-tuple-element.73), channel_id=1, source_target_pairs={{0,4},{4,0},{8,12},{12,8},{1,5},{5,1},{9,13},{13,9},{2,6},{6,2},{1... | collective-permute-start | bytes 3538952 | tf_op jit(solution)/shard_map/ppermute | solution.py:216
  83.6 7.4 %collective-permute-start.4 = (bf16[64,1152]{1,0:T(8,128)(2,1)S(1)}, bf16[64,1152]{1,0:T(8,128)(2,1)S(1)}, u32[]{:S(2)}, u32[]{:S(2)}) collective-permute-start(bf16[64,1152]{1,0:T(8,128)(2,1)S(1)} %shard_map.84), channel_id=1, source_target_pairs={{16,0},{32,16},{48,32},{64,48},{80,64},{96,80},{112,96},{128,112},... | collective-permute-start | bytes 442376 | tf_op jit(solution)/shard_map/ppermute | solution.py:220
  85.1 16.3 %copy-start.3 = (bf16[2,128,2304]{2,1,0:T(8,128)(2,1)S(1)}, bf16[2,128,2304]{2,1,0:T(8,128)(2,1)}, u32[]{:S(2)}) copy-start(bf16[2,128,2304]{2,1,0:T(8,128)(2,1)} %top_ref.3) | copy-start | bytes 3538948
  85.1 17.8 %collective-permute-start.6 = (bf16[576,512]{1,0:T(8,128)(2,1)S(1)}, bf16[576,512]{1,0:T(8,128)(2,1)S(1)}, u32[]{:S(2)}, u32[]{:S(2)}) collective-permute-start(bf16[576,512]{1,0:T(8,128)(2,1)S(1)} %fusion.1), channel_id=1, source_target_pairs={{0,8},{4,12},{8,0},{12,4},{1,9},{5,13},{9,1},{13,5},{2,10},{6,14},... | collective-permute-start | bytes 1769480 | tf_op jit(solution)/shard_map/ppermute | solution.py:216

commit v5 on v4

--- a/solution.py
+++ b/solution.py
@@ -139,8 +139,8 @@
     act_ref[...] = activated.astype(bf16)
     hidden_ref[...] = hidden
     slope_ref[...] = slope
-    for j in range(acc_ref.shape[0]):
-        acc_ref[j] = dot_tn(left_ref[lax.bitwise_xor(fsdp, j)], right_ref[...])
+    for n in range(acc_ref.shape[0]):
+        acc_ref[n] = dot_tn(left_ref[lax.bitwise_xor(fsdp, 2 * n + 1)], right_ref[...])
 
 
 def second_kernel(
@@ -184,17 +184,22 @@
     out_ref[:, width:] = share[rows:]
 
 
-def late_kernel(h_ref, dy_ref, pre_ref, act_ref, acc_ref, keep_ref, send_ref):
+def late_kernel(h_ref, dy_ref, pre_ref, act_ref, acc_ref, send_ref):
     fsdp = lax.axis_index("fsdp")
     right = jnp.concatenate([pre_ref[...], act_ref[...]], axis=0)
-    for j in range(acc_ref.shape[0]):
-        block = lax.bitwise_xor(fsdp, j)
+    for n in range(send_ref.shape[0]):
+        block = lax.bitwise_xor(fsdp, 2 * n + 1)
         left = jnp.concatenate([h_ref[block], dy_ref[block]], axis=0)
-        total = acc_ref[j] + dot_tn(left, right)
-        if j % 2:
-            send_ref[j // 2] = total.astype(bf16)
-        else:
-            keep_ref[j // 2] = total
+        send_ref[n] = (acc_ref[n] + dot_tn(left, right)).astype(bf16)
+
+
+def stay_kernel(left_ref, right_ref, h_ref, dy_ref, pre_ref, act_ref, keep_ref):
+    fsdp = lax.axis_index("fsdp")
+    right = jnp.concatenate([pre_ref[...], act_ref[...]], axis=0)
+    for n in range(keep_ref.shape[0]):
+        block = lax.bitwise_xor(fsdp, 2 * n)
+        left = jnp.concatenate([h_ref[block], dy_ref[block]], axis=0)
+        keep_ref[n] = dot_tn(left_ref[block], right_ref[...]) + dot_tn(left, right)
 
 
 def last_kernel(got_ref, top_ref, held_ref):
@@ -269,9 +274,9 @@
             compiler_params=pltpu.CompilerParams(vmem_limit_bytes=vmem_budget),
         )(order, stash, gain, extra)
 
+    pair = (tp_count // 2, width, inner)
     w0 = weight[0]
     w2 = swapped(w0, "fsdp", 2)
-    w1 = swapped(w0, "fsdp", 1)
     one = (1, tokens, features)
     left1, x1, inv1, dy1, gains = prepared(
         prepare_first_kernel, 0, grad_now, one, [pairs, own, stats, own, gain_own]
@@ -279,6 +284,8 @@
     h2, x2, inv2, top1 = prepared(
         prepare_second_kernel, 1, grad_top, one, [blocks, own, stats, blocks]
     )
+    (w0_late, left1) = lax.optimization_barrier((w0, left1))
+    w1 = swapped(w0_late, "fsdp", 1)
     (w2, left1, x1, inv1, dy1, gains, h2, x2, inv2, top1) = lax.optimization_barrier(
         (w2, left1, x1, inv1, dy1, gains, h2, x2, inv2, top1)
     )
@@ -295,7 +302,7 @@
     acc, act2, hidden2, slope2 = call(
         between_kernel,
         3 * dot,
-        [sds((tp_count, width, inner), f32), flat, high, high],
+        [sds(pair, f32), flat, high, high],
         left1, right1, h2, *weights,
     )
     (arrived1, acc, act2, hidden2, slope2) = lax.optimization_barrier(
@@ -311,14 +318,10 @@
     got2 = exchanged(out2)
     share2 = call(own_share, dot // 8, share, got2, x2, inv2, gains, dy2_own)
     arrived2 = moved_down(share2)
-    pair = (tp_count // 2, width, inner)
-    keep, send = call(
-        late_kernel,
-        2 * dot,
-        [sds(pair, f32), sds(pair, bf16)],
-        h2, dy2, pre2, act2, acc,
-    )
+    late_args = (h2, dy2, pre2, act2)
+    send = call(late_kernel, dot, sds(pair, bf16), *late_args, acc)
     from_core = swapped(send, "fsdp", 1)
+    keep = call(stay_kernel, 2 * dot, sds(pair, f32), left1, right1, *late_args)
     across = keep[1] + from_core[1].astype(f32)
     across = swapped(across.astype(bf16), "fsdp", 2)
     held2 = copied_to_all(arrived2)

time: 105 us -> 115 us (1.095)
  blocking collectives: 46.4 us -> 33.6 us
  local copies, waits for them, and re-layouts: 4.38 us -> 12 us
  waiting for transfers between devices: 9.55 us -> 15.5 us
  starting transfers between devices: 32 us -> 36.2 us
  other arithmetic: 1.42 us -> 3.92 us
  Pallas kernels: 9.5 us -> 11.8 us
    all_to_all x4 -> x3, blocking collectives: 46.4 us -> 33.6 us  [exchanged(): return lax.all_to_all(values, 'tp', split_axis=0, concat_axis=0, tiled=True)]
    unnamed x14 -> x40, local copies, waits for them, and re-layouts: 4.3 us -> 11.9 us
    all_to_all x0 -> x1, waiting for transfers between devices: none -> 6.8 us  [exchanged(): return lax.all_to_all(values, 'tp', split_axis=0, concat_axis=0, tiled=True)]
    all_to_all x0 -> x1, starting transfers between devices: none -> 4.17 us  [exchanged(): return lax.all_to_all(values, 'tp', split_axis=0, concat_axis=0, tiled=True)]
    pallas_call x8 -> x9, Pallas kernels: 7.37 us -> 9.66 us  [call(): pl.pallas_call(kernel, out_shape=outs, cost_estimate=cost(flops, outs, ar...]
    convert_element_type x1, other arithmetic: 0.19 us -> 1.61 us  [per_device(): across = swapped(across.astype(bf16), 'fsdp', 2)]
  transfers between devices with their start and end apart: 7 -> 8, of which waited for: 4 -> 4; matrix products, arithmetic and copies ran while one was open for 0% -> 1% of each run, Pallas kernels for 5% -> 6%
where the time goes in v5:
time: 115 us; the launch traced here: 114 us
  starting transfers between devices  36.2 us (31%)
  blocking collectives  33.6 us (29%)
  waiting for transfers between devices  15.5 us (13%)
  local copies, waits for them, and re-layouts  12 us (10%)
  Pallas kernels  11.8 us (10%)
  other arithmetic  3.92 us (3%)
    all_to_all x3, blocking collectives, exchanged(): return lax.all_to_all(values, 'tp', split_axis=0, concat_axis=0, tiled=True)  33.6 us
    ppermute x5, starting transfers between devices, swapped(): lax.ppermute(values, axis, [(i, i ^ bit) for i in range(lax.axis_size(axi...  29.5 us
    unnamed x40, local copies, waits for them, and re-layouts  11.9 us
    pallas_call x9, Pallas kernels, call(): pl.pallas_call(kernel, out_shape=outs, cost_estimate=cost(flops, outs, ar...  9.66 us
    ppermute x2, waiting for transfers between devices, moved_down(): lax.ppermute(values, 'section', [(i, i - 1) for i in range(1, lax.axis_si...  7.93 us
    all_to_all x1, waiting for transfers between devices, exchanged(): return lax.all_to_all(values, 'tp', split_axis=0, concat_axis=0, tiled=True)  6.8 us
    all_to_all x1, starting transfers between devices, exchanged(): return lax.all_to_all(values, 'tp', split_axis=0, concat_axis=0, tiled=True)  4.17 us
    ppermute x2, starting transfers between devices, moved_down(): lax.ppermute(values, 'section', [(i, i - 1) for i in range(1, lax.axis_si...  2.58 us
  transfers between devices with their start and end apart: 8, of which 4 were waited for; matrix products, arithmetic and copies ran while one was open for 1% of the time, Pallas kernels for 6%

profile of v5, /device:TPU:1, one launch (start us, length us, event | category | flops | bytes accessed | tf_op | source)
XLA Modules:
  0.0 114.0 jit_solution(2345195895857567629)
XLA Ops:
  0.6 0.0 copy-start
  0.6 4.2 %collective-permute-start = (bf16[576,512]{1,0:T(8,128)(2,1)}, bf16[576,512]{1,0:T(8,128)(2,1)S(1)}, u32[]{:S(2)}, u32[]{:S(2)}) collective-permute-start(bf16[576,512]{1,0:T(8,128)(2,1)} %bitcast.11), channel_id=1, source_target_pairs={{0,8},{4,12},{8,0},{12,4},{1,9},{5,13},{9,1},{13,5},{2,10},{6,14},... | collective-permute-start | bytes 1769480 | tf_op jit(solution)/shard_map/ppermute | solution.py:221
  4.8 0.0 copy-start.1
  4.8 1.7 %copy-done.1 = bf16[1,4,128,2304]{3,2,1,0:T(8,128)(2,1)S(1)} copy-done((bf16[1,4,128,2304]{3,2,1,0:T(8,128)(2,1)S(1)}, bf16[1,4,128,2304]{3,2,1,0:T(8,128)(2,1)}, u32[]{:S(2)}) %copy-start.1) | copy-done | bytes 2359320
  6.5 0.0 copy-start.8
  6.5 1.1 copy-done.8
  7.5 0.0 copy-start.17
  7.5 0.7 copy-done.17
  8.2 0.0 copy-start.19
  8.2 0.7 copy-done.19
  8.9 0.0 copy-start.4
  8.9 0.0 copy-start.18
  8.9 1.1 shard_map.77
  10.0 0.0 copy-done
  10.0 13.9 %collective-permute-start.1 = (bf16[576,512]{1,0:T(8,128)(2,1)S(1)}, bf16[576,512]{1,0:T(8,128)(2,1)S(1)}, u32[]{:S(2)}, u32[]{:S(2)}) collective-permute-start(bf16[576,512]{1,0:T(8,128)(2,1)S(1)} %bitcast.12), channel_id=1, source_target_pairs={{0,4},{4,0},{8,12},{12,8},{1,5},{5,1},{9,13},{13,9},{2,6},{6,2},{1... | collective-permute-start | bytes 1769480 | tf_op jit(solution)/shard_map/ppermute | solution.py:221
  23.9 0.0 copy-done.4
  23.9 0.0 copy-done.18
  23.9 1.1 shard_map.78
  25.0 0.0 copy-start.11
  25.0 0.0 copy-start.15
  25.0 0.0 collective-permute-done.w2
  25.0 3.8 %collective-permute-start.2 = (bf16[576,512]{1,0:T(8,128)(2,1)S(1)}, bf16[576,512]{1,0:T(8,128)(2,1)S(1)}, u32[]{:S(2)}, u32[]{:S(2)}) collective-permute-start(bf16[576,512]{1,0:T(8,128)(2,1)S(1)} %collective-permute-done.w2), channel_id=1, source_target_pairs={{0,4},{4,0},{8,12},{12,8},{1,5},{5,1},{9,13},{13,9},{2,6},{6,2},{1... | collective-permute-start | bytes 1769480 | tf_op jit(solution)/shard_map/ppermute | solution.py:221
  28.8 0.0 collective-permute-done.1.w1
  28.8 0.8 shard_map.79.part_ref
  29.6 0.0 copy-done.11
  29.6 0.0 copy-done.15
  29.6 0.8 collective-permute-done.2.w3
  30.4 1.3 %shard_map.80 = (bf16[256,512]{1,0:T(8,128)(2,1)S(1)}, bf16[4,128,640]{2,1,0:T(8,128)(2,1)S(1)}) custom-call(f32[256,512]{1,0:T(8,128)S(1)} %shard_map.79.part_ref, bf16[4,256,576]{2,1,0:T(8,128)(2,1)S(1)} %get-tuple-element.48.left_ref, bf16[576,512]{1,0:T(8,128)(2,1)S(1)} %bitcast.14, bf16[576,512]{1,0:T(8,128)(2,1)S(1)} %collective-permute-done.1.w1, ...), custom_call_target="tpu_custom_call" | custom-call | flops 603979776 | bytes 4980736 | tf_op jit(solution)/shard_map/pallas_call | solution.py:47
  31.7 13.0 %all_to_all.20.got_ref = bf16[4,128,640]{2,1,0:T(8,128)(2,1)S(1)} all-to-all(bf16[4,128,640]{2,1,0:T(8,128)(2,1)S(1)} %get-tuple-element.51), channel_id=1, replica_groups=mesh['section'=64,'fsdp'=4,'tp'=4] {'tp'}, dimensions={0} | all-to-all | bytes 1310720 | tf_op jit(solution)/shard_map/all_to_all | solution.py:231
  44.7 0.3 shard_map.81
  45.0 1.3 %collective-permute-start.3 = (bf16[64,1152]{1,0:T(8,128)(2,1)S(1)}, bf16[64,1152]{1,0:T(8,128)(2,1)S(1)}, u32[]{:S(2)}, u32[]{:S(2)}) collective-permute-start(bf16[64,1152]{1,0:T(8,128)(2,1)S(1)} %shard_map.81), channel_id=1, source_target_pairs={{16,0},{32,16},{48,32},{64,48},{80,64},{96,80},{112,96},{128,112},... | collective-permute-start | bytes 442376 | tf_op jit(solution)/shard_map/ppermute | solution.py:225
  46.3 1.0 shard_map.82
  47.3 5.1 %collective-permute-done.3 = bf16[64,1152]{1,0:T(8,128)(2,1)S(1)} collective-permute-done((bf16[64,1152]{1,0:T(8,128)(2,1)S(1)}, bf16[64,1152]{1,0:T(8,128)(2,1)S(1)}, u32[]{:S(2)}, u32[]{:S(2)}) %collective-permute-start.3) | collective-permute-done | bytes 147488 | tf_op jit(solution)/shard_map/ppermute | solution.py:225
  52.5 10.0 %all_to_all.21.got_ref = bf16[4,64,1152]{2,1,0:T(8,128)(2,1)S(1)} all-to-all(bf16[4,64,1152]{2,1,0:T(8,128)(2,1)S(1)} %broadcast_in_dim.9), channel_id=1, replica_groups=mesh['section'=64,'fsdp'=4,'tp'=4] {'tp'}, dimensions={0} | all-to-all | bytes 1179648 | tf_op jit(solution)/shard_map/all_to_all | solution.py:231
  62.5 1.6 %shard_map.83 = (bf16[4,128,576]{2,1,0:T(8,128)(2,1)S(1)}, bf16[128,512]{1,0:T(8,128)(2,1)S(1)}, bf16[4,128,640]{2,1,0:T(8,128)(2,1)S(1)}, bf16[128,576]{1,0:T(8,128)(2,1)S(1)}) custom-call(f32[128,512]{1,0:T(8,128)S(1)} %get-tuple-element.62.hidden_ref, f32[128,512]{1,0:T(8,128)S(1)} %get-tuple-element.63.slope_ref, ...), custom_call_target="tpu_custom_call" | custom-call | flops 603979776 | bytes 5586944 | tf_op jit(solution)/shard_map/pallas_call | solution.py:47
  64.1 0.0 copy-start.7
  64.1 0.8 copy-done.7
  64.9 1.5 %shard_map.87 = bf16[2,576,512]{2,1,0:T(8,128)(2,1)} custom-call(bf16[4,128,576]{2,1,0:T(8,128)(2,1)S(1)} %get-tuple-element.57.h_ref, bf16[4,128,576]{2,1,0:T(8,128)(2,1)S(1)} %get-tuple-element.70.dy_ref, bf16[128,512]{1,0:T(8,128)(2,1)S(1)} %get-tuple-element.71.pre_ref, bf16[128,512]{1,0:T(8,128)(2,1)S(1)} %get-tuple-element.72.act_ref, ...), custom_call_target="tpu_custom_call" | custom-call | flops 301989888 | bytes 4980736 | tf_op jit(solution)/shard_map/pallas_call | solution.py:47
  66.4 0.0 copy-done.5
  66.4 0.0 copy-done.9
  66.4 0.0 copy-done.13
  66.4 5.4 %collective-permute-start.5 = (bf16[2,576,512]{2,1,0:T(8,128)(2,1)}, bf16[2,576,512]{2,1,0:T(8,128)(2,1)}, u32[]{:S(2)}, u32[]{:S(2)}) collective-permute-start(bf16[2,576,512]{2,1,0:T(8,128)(2,1)} %shard_map.87), channel_id=1, source_target_pairs={{0,4},{4,0},{8,12},{12,8},{1,5},{5,1},{9,13},{13,9},{2,6},{6,2},{1... | collective-permute-start | bytes 3538952 | tf_op jit(solution)/shard_map/ppermute | solution.py:221
  71.9 4.2 %all-to-all-start.2 = ((bf16[4,128,640]{2,1,0:T(8,128)(2,1)}), bf16[4,128,640]{2,1,0:T(8,128)(2,1)}, u32[]{:S(2)}, u32[]{:S(2)}) async-start(bf16[4,128,640]{2,1,0:T(8,128)(2,1)} %copy-done.7), calls=%async_computation.2 | async-start | bytes 1310720 | tf_op jit(solution)/shard_map/all_to_all | solution.py:231
  76.1 0.0 copy-start.6
  76.1 1.1 copy-done.6
  77.2 0.9 copy-done.10
  78.1 0.8 shard_map.86
  78.9 0.0 copy-start.2
  78.9 1.4 %copy-done.2 = f32[2,576,512]{2,1,0:T(8,128)} copy-done((f32[2,576,512]{2,1,0:T(8,128)}, f32[2,576,512]{2,1,0:T(8,128)S(1)}, u32[]{:S(2)}) %copy-start.2) | copy-done | bytes 2359320
  80.3 6.8 %all-to-all-done.2.got_ref = bf16[4,128,640]{2,1,0:T(8,128)(2,1)} async-done(((bf16[4,128,640]{2,1,0:T(8,128)(2,1)}), bf16[4,128,640]{2,1,0:T(8,128)(2,1)}, u32[]{:S(2)}, u32[]{:S(2)}) %all-to-all-start.2) | async-done | bytes 655392 | tf_op jit(solution)/shard_map/all_to_all | solution.py:231
  87.1 0.9 copy-done.12
  88.0 0.9 copy-done.14
  88.9 0.8 copy-done.16
  89.8 1.4 %shard_map.84 = bf16[64,1152]{1,0:T(8,128)(2,1)S(1)} custom-call(bf16[4,128,640]{2,1,0:T(8,128)(2,1)} %all-to-all-done.2.got_ref, bf16[128,576]{1,0:T(8,128)(2,1)S(1)} %copy-done.12, f32[128,128]{1,0:T(8,128)S(1)} %copy-done.16, f32[1,576]{1,0:T(1,128)S(1)} %get-tuple-element.54.gain_ref, bf16[128,576]{1,0:T(8,128)(2,1)S(1)} %copy-done.14), custom_call_target="tpu_custom_call" | custom-call | flops 37748736 | bytes 1165568 | tf_op jit(solution)/shard_map/pallas_call | solution.py:47
  91.2 1.3 %collective-permute-start.4 = (bf16[64,1152]{1,0:T(8,128)(2,1)S(1)}, bf16[64,1152]{1,0:T(8,128)(2,1)S(1)}, u32[]{:S(2)}, u32[]{:S(2)}) collective-permute-start(bf16[64,1152]{1,0:T(8,128)(2,1)S(1)} %shard_map.84), channel_id=1, source_target_pairs={{16,0},{32,16},{48,32},{64,48},{80,64},{96,80},{112,96},{128,112},... | collective-permute-start | bytes 442376 | tf_op jit(solution)/shard_map/ppermute | solution.py:225
  92.5 0.0 collective-permute-done.5
  92.5 1.6 %fusion.4 = bf16[576,512]{1,0:T(8,128)(2,1)S(1)} fusion(f32[2,576,512]{2,1,0:T(8,128)} %copy-done.2, bf16[2,576,512]{2,1,0:T(8,128)(2,1)} %collective-permute-done.5), kind=kLoop, calls=%fused_computation.6 | loop fusion | flops 884736 | bytes 2359296 | tf_op jit(solution)/shard_map/convert_element_type | solution.py:326
  94.1 2.2 %collective-permute-start.6 = (bf16[576,512]{1,0:T(8,128)(2,1)S(1)}, bf16[576,512]{1,0:T(8,128)(2,1)S(1)}, u32[]{:S(2)}, u32[]{:S(2)}) collective-permute-start(bf16[576,512]{1,0:T(8,128)(2,1)S(1)} %fusion.4), channel_id=1, source_target_pairs={{0,8},{4,12},{8,0},{12,4},{1,9},{5,13},{9,1},{13,5},{2,10},{6,14},... | collective-permute-start | bytes 1769480 | tf_op jit(solution)/shard_map/ppermute | solution.py:221
  96.3 2.8 %collective-permute-done.4 = bf16[64,1152]{1,0:T(8,128)(2,1)S(1)} collective-permute-done((bf16[64,1152]{1,0:T(8,128)(2,1)S(1)}, bf16[64,1152]{1,0:T(8,128)(2,1)S(1)}, u32[]{:S(2)}, u32[]{:S(2)}) %collective-permute-start.4) | collective-permute-done | bytes 147488 | tf_op jit(solution)/shard_map/ppermute | solution.py:225
  99.1 10.6 %all_to_all.22.got_ref = bf16[4,64,1152]{2,1,0:T(8,128)(2,1)S(1)} all-to-all(bf16[4,64,1152]{2,1,0:T(8,128)(2,1)S(1)} %broadcast_in_dim.10), channel_id=1, replica_groups=mesh['section'=64,'fsdp'=4,'tp'=4] {'tp'}, dimensions={0} | all-to-all | bytes 1179648 | tf_op jit(solution)/shard_map/all_to_all | solution.py:231
  109.8 1.0 shard_map.85
  110.8 0.0 collective-permute-done.6
  110.8 0.9 copy-done.3
  111.7 2.3 %fusion.3 = f32[1,576,512]{2,1,0:T(8,128)} fusion(f32[2,576,512]{2,1,0:T(8,128)S(1)} %copy-done.3, bf16[576,512]{1,0:T(8,128)(2,1)S(1)} %collective-permute-done.6, bf16[2,576,512]{2,1,0:T(8,128)(2,1)} %collective-permute-done.5), kind=kLoop, calls=%fused_computation.5 | loop fusion | flops 1179648 | bytes 3538944 | tf_op jit(solution)/shard_map/broadcast_in_dim | solution.py:330
  (10 shorter events, 0.1 us)
Async XLA Ops:
  0.6 9.3 %copy-start = (bf16[1,576,512]{2,1,0:T(8,128)(2,1)S(1)}, bf16[1,576,512]{2,1,0:T(8,128)(2,1)}, u32[]{:S(2)}) copy-start(bf16[1,576,512]{2,1,0:T(8,128)(2,1)} %param.11) | copy-start | bytes 1769476
  0.6 24.4 %collective-permute-start = (bf16[576,512]{1,0:T(8,128)(2,1)}, bf16[576,512]{1,0:T(8,128)(2,1)S(1)}, u32[]{:S(2)}, u32[]{:S(2)}) collective-permute-start(bf16[576,512]{1,0:T(8,128)(2,1)} %bitcast.11), channel_id=1, source_target_pairs={{0,8},{4,12},{8,0},{12,4},{1,9},{5,13},{9,1},{13,5},{2,10},{6,14},... | collective-permute-start | bytes 1769480 | tf_op jit(solution)/shard_map/ppermute | solution.py:221
  4.8 1.7 %copy-start.1 = (bf16[1,4,128,2304]{3,2,1,0:T(8,128)(2,1)S(1)}, bf16[1,4,128,2304]{3,2,1,0:T(8,128)(2,1)}, u32[]{:S(2)}) copy-start(bf16[1,4,128,2304]{3,2,1,0:T(8,128)(2,1)} %stash_ref.3) | copy-start | bytes 7077892
  6.5 1.1 copy-start.8
  7.5 0.7 copy-start.17
  8.2 0.7 copy-start.19
  8.9 15.0 %copy-start.4 = (bf16[2,128,2304]{2,1,0:T(8,128)(2,1)S(1)}, bf16[2,128,2304]{2,1,0:T(8,128)(2,1)}, u32[]{:S(2)}) copy-start(bf16[2,128,2304]{2,1,0:T(8,128)(2,1)} %top_ref.3) | copy-start | bytes 3538948
  8.9 15.0 %copy-start.18 = (f32[1,2304]{1,0:T(1,128)S(1)}, f32[1,2304]{1,0:T(1,128)}, u32[]{:S(2)}) copy-start(f32[1,2304]{1,0:T(1,128)} %gain_ref.3) | copy-start | bytes 27652
  10.0 18.8 %collective-permute-start.1 = (bf16[576,512]{1,0:T(8,128)(2,1)S(1)}, bf16[576,512]{1,0:T(8,128)(2,1)S(1)}, u32[]{:S(2)}, u32[]{:S(2)}) collective-permute-start(bf16[576,512]{1,0:T(8,128)(2,1)S(1)} %bitcast.12), channel_id=1, source_target_pairs={{0,4},{4,0},{8,12},{12,8},{1,5},{5,1},{9,13},{13,9},{2,6},{6,2},{1... | collective-permute-start | bytes 1769480 | tf_op jit(solution)/shard_map/ppermute | solution.py:221
  25.0 4.6 %copy-start.11 = (bf16[128,576]{1,0:T(8,128)(2,1)}, bf16[128,576]{1,0:T(8,128)(2,1)S(1)}, u32[]{:S(2)}) copy-start(bf16[128,576]{1,0:T(8,128)(2,1)S(1)} %get-tuple-element.67.x_ref) | copy-start | bytes 442372
  25.0 4.6 %copy-start.15 = (f32[128,128]{1,0:T(8,128)}, f32[128,128]{1,0:T(8,128)S(1)}, u32[]{:S(2)}) copy-start(f32[128,128]{1,0:T(8,128)S(1)} %get-tuple-element.68.inv_ref) | copy-start | bytes 196612
  25.0 5.4 %collective-permute-start.2 = (bf16[576,512]{1,0:T(8,128)(2,1)S(1)}, bf16[576,512]{1,0:T(8,128)(2,1)S(1)}, u32[]{:S(2)}, u32[]{:S(2)}) collective-permute-start(bf16[576,512]{1,0:T(8,128)(2,1)S(1)} %collective-permute-done.w2), channel_id=1, source_target_pairs={{0,4},{4,0},{8,12},{12,8},{1,5},{5,1},{9,13},{13,9},{2,6},{6,2},{1... | collective-permute-start | bytes 1769480 | tf_op jit(solution)/shard_map/ppermute | solution.py:221
  45.0 7.4 %collective-permute-start.3 = (bf16[64,1152]{1,0:T(8,128)(2,1)S(1)}, bf16[64,1152]{1,0:T(8,128)(2,1)S(1)}, u32[]{:S(2)}, u32[]{:S(2)}) collective-permute-start(bf16[64,1152]{1,0:T(8,128)(2,1)S(1)} %shard_map.81), channel_id=1, source_target_pairs={{16,0},{32,16},{48,32},{64,48},{80,64},{96,80},{112,96},{128,112},... | collective-permute-start | bytes 442376 | tf_op jit(solution)/shard_map/ppermute | solution.py:225
  64.1 0.8 copy-start.7
  64.9 1.5 %copy-start.5 = (bf16[4,128,576]{2,1,0:T(8,128)(2,1)}, bf16[4,128,576]{2,1,0:T(8,128)(2,1)S(1)}, u32[]{:S(2)}) copy-start(bf16[4,128,576]{2,1,0:T(8,128)(2,1)S(1)} %get-tuple-element.70.dy_ref) | copy-start | bytes 1769476
  64.9 1.5 %copy-start.9 = (bf16[128,512]{1,0:T(8,128)(2,1)}, bf16[128,512]{1,0:T(8,128)(2,1)S(1)}, u32[]{:S(2)}) copy-start(bf16[128,512]{1,0:T(8,128)(2,1)S(1)} %get-tuple-element.71.pre_ref) | copy-start | bytes 393220
  64.9 1.5 %copy-start.13 = (bf16[128,576]{1,0:T(8,128)(2,1)}, bf16[128,576]{1,0:T(8,128)(2,1)S(1)}, u32[]{:S(2)}) copy-start(bf16[128,576]{1,0:T(8,128)(2,1)S(1)} %get-tuple-element.69.dy_ref) | copy-start | bytes 442372
  66.4 26.0 %collective-permute-start.5 = (bf16[2,576,512]{2,1,0:T(8,128)(2,1)}, bf16[2,576,512]{2,1,0:T(8,128)(2,1)}, u32[]{:S(2)}, u32[]{:S(2)}) collective-permute-start(bf16[2,576,512]{2,1,0:T(8,128)(2,1)} %shard_map.87), channel_id=1, source_target_pairs={{0,4},{4,0},{8,12},{12,8},{1,5},{5,1},{9,13},{13,9},{2,6},{6,2},{1... | collective-permute-start | bytes 3538952 | tf_op jit(solution)/shard_map/ppermute | solution.py:221
  71.9 15.2 %all-to-all-start.2 = ((bf16[4,128,640]{2,1,0:T(8,128)(2,1)}), bf16[4,128,640]{2,1,0:T(8,128)(2,1)}, u32[]{:S(2)}, u32[]{:S(2)}) async-start(bf16[4,128,640]{2,1,0:T(8,128)(2,1)} %copy-done.7), calls=%async_computation.2 | async-start | bytes 1310720 | tf_op jit(solution)/shard_map/all_to_all | solution.py:231
  76.1 1.1 copy-start.6
  77.2 0.9 copy-start.10
  78.9 1.4 %copy-start.2 = (f32[2,576,512]{2,1,0:T(8,128)}, f32[2,576,512]{2,1,0:T(8,128)S(1)}, u32[]{:S(2)}) copy-start(f32[2,576,512]{2,1,0:T(8,128)S(1)} %shard_map.86) | copy-start | bytes 7077892
  87.1 0.9 copy-start.12
  88.0 0.9 copy-start.14
  88.9 0.8 copy-start.16
  91.2 7.9 %collective-permute-start.4 = (bf16[64,1152]{1,0:T(8,128)(2,1)S(1)}, bf16[64,1152]{1,0:T(8,128)(2,1)S(1)}, u32[]{:S(2)}, u32[]{:S(2)}) collective-permute-start(bf16[64,1152]{1,0:T(8,128)(2,1)S(1)} %shard_map.84), channel_id=1, source_target_pairs={{16,0},{32,16},{48,32},{64,48},{80,64},{96,80},{112,96},{128,112},... | collective-permute-start | bytes 442376 | tf_op jit(solution)/shard_map/ppermute | solution.py:225
  94.1 16.7 %collective-permute-start.6 = (bf16[576,512]{1,0:T(8,128)(2,1)S(1)}, bf16[576,512]{1,0:T(8,128)(2,1)S(1)}, u32[]{:S(2)}, u32[]{:S(2)}) collective-permute-start(bf16[576,512]{1,0:T(8,128)(2,1)S(1)} %fusion.4), channel_id=1, source_target_pairs={{0,8},{4,12},{8,0},{12,4},{1,9},{5,13},{9,1},{13,5},{2,10},{6,14},... | collective-permute-start | bytes 1769480 | tf_op jit(solution)/shard_map/ppermute | solution.py:221
  109.8 1.9 %copy-start.3 = (f32[2,576,512]{2,1,0:T(8,128)S(1)}, f32[2,576,512]{2,1,0:T(8,128)}, u32[]{:S(2)}) copy-start(f32[2,576,512]{2,1,0:T(8,128)} %copy-done.2) | copy-start | bytes 7077892
